TPU v7x, 32 devices: a whole 2x2x4 slice. The times are simulated.
32 devices in a mesh: group: 2 (over x), expert: 16 (over z, y, core).
Axes of the slice: x: 2, y: 2, z: 4, core: 2. Of those that a mesh axis runs over, the one named last changes fastest.
Arguments:
- query: bfloat16 [32, 2048], P(('group', 'expert')), parts along dimension 0, may hold values from -600 to 600
- key_new: bfloat16 [32, 2048], P(('group', 'expert')), parts along dimension 0, may hold values from -6 to 6
- value_new: bfloat16 [32, 2048], P(('group', 'expert')), parts along dimension 0, may hold values from -6 to 6
- key_cache: bfloat16 [32, 256, 2048], P(('group', 'expert')), parts along dimension 0, may hold values from -6 to 6
- value_cache: bfloat16 [32, 256, 2048], P(('group', 'expert')), parts along dimension 0, may hold values from -6 to 6
- lengths: int32 [32], P(('group', 'expert')), parts along dimension 0, may hold values from 1 to 256
- hidden: bfloat16 [32, 2048], P(('group', 'expert')), parts along dimension 0, may hold values from -6 to 6
- routes: int32 [32], P('group'), parts along dimension 0, may hold values from 0 to 31, as said below
- w_out: bfloat16 [2048, 2048], P(None, 'expert'), may hold values from -0.125 to 0.125
- ln_gain: bfloat16 [2048], replicated, may hold values from 0.099609375 to 1.8984375
- router: bfloat16 [2048, 32], replicated, may hold values from -0.125 to 0.125
- shared_up: bfloat16 [2048, 8192], P(None, 'expert'), may hold values from -0.125 to 0.125
- shared_down: bfloat16 [8192, 2048], P('expert'), may hold values from -0.0625 to 0.0625
- expert_up: bfloat16 [2048, 131072], P(None, 'expert'), may hold values from -0.125 to 0.125
- expert_down: bfloat16 [131072, 2048], P('expert'), may hold values from -0.09375 to 0.09375
Outputs:
- layer_out: bfloat16 [32, 2048], P(('group', 'expert')), parts along dimension 0
There are 2 independent parts, one for each index of `group`. A program takes and returns all parts, laid end to end along the dimension named above; an argument that names none is the same for every part. Nothing has to cross between parts.
Inputs may be any that keep to these rules, and one draw needn't show every extreme that they name: `routes`: no expert is named by more than 2 tokens of the group, and in every draw some expert is named by exactly 2.
All inputs are finite; a program needn't handle non-finite values.
Results may differ from a plain program's by a relative error of at most 0.0085.
Values may be sent and summed in bfloat16 or wider, within the bound.
No kernel may reach another device: no remote copies, remote signals or barrier semaphores. Data moves between devices by JAX's collectives and lax.ppermute only.
A program may use at most 128 MiB of HBM per device.

v0:
```python
import math

import jax
import jax.numpy as jnp
from jax import lax
from jax.sharding import PartitionSpec as P

D = 2048
HEADS = 16
HEAD_DIM = 128
FF = 4096
EXPERTS = 32


def attend(query, key_new, value_new, key_cache, value_cache, lengths):
    seq_count = query.shape[0]
    cache_len = key_cache.shape[1]
    scale_factor = 1.0 / math.sqrt(HEAD_DIM)
    head_query = query.reshape(seq_count, HEADS, HEAD_DIM)
    head_keys = key_cache.reshape(seq_count, cache_len, HEADS, HEAD_DIM)
    head_values = value_cache.reshape(seq_count, cache_len, HEADS, HEAD_DIM)
    scores = (
        jnp.einsum("shd,schd->shc", head_query, head_keys, preferred_element_type=jnp.float32)
        * scale_factor
    )
    own_score = (
        jnp.einsum(
            "shd,shd->sh",
            head_query,
            key_new.reshape(seq_count, HEADS, HEAD_DIM),
            preferred_element_type=jnp.float32,
        )
        * scale_factor
    )
    positions = jnp.arange(cache_len, dtype=jnp.int32)
    scores = jnp.where(positions[None, None, :] < lengths[:, None, None], scores, -1e30)
    top_score = jnp.maximum(jnp.max(scores, axis=2), own_score)
    weights = jnp.exp(scores - top_score[:, :, None])
    own_weight = jnp.exp(own_score - top_score)
    normalizer = jnp.sum(weights, axis=2) + own_weight
    weights = (weights / normalizer[:, :, None]).astype(jnp.bfloat16)
    own_weight = (own_weight / normalizer).astype(jnp.bfloat16)
    mixed_values = jnp.einsum(
        "shc,schd->shd", weights, head_values, preferred_element_type=jnp.float32
    )
    mixed_values = mixed_values + own_weight.astype(jnp.float32)[:, :, None] * value_new.reshape(
        seq_count, HEADS, HEAD_DIM
    ).astype(jnp.float32)
    return mixed_values.reshape(seq_count, HEADS * HEAD_DIM).astype(jnp.bfloat16)


def body(
    query,
    key_new,
    value_new,
    key_cache,
    value_cache,
    lengths,
    hidden,
    routes,
    w_out,
    ln_gain,
    router,
    shared_up,
    shared_down,
    expert_up,
    expert_down,
):
    seq_count = query.shape[0]
    attended = attend(query, key_new, value_new, key_cache, value_cache, lengths)
    every_attended, every_hidden = (
        lax.all_gather(attended, "expert", axis=0, tiled=True),
        lax.all_gather(hidden, "expert", axis=0, tiled=True),
    )
    projected = jnp.dot(every_attended, w_out, preferred_element_type=jnp.float32).astype(
        jnp.bfloat16
    )
    every_projected = lax.all_gather(projected, "expert", axis=1, tiled=True)
    residual = every_hidden.astype(jnp.float32) + every_projected.astype(jnp.float32)
    centered = residual - jnp.mean(residual, axis=1, keepdims=True)
    variance = jnp.mean(centered * centered, axis=1, keepdims=True)
    normed = (
        centered / jnp.sqrt(jnp.maximum(variance, 0.25)) * ln_gain.astype(jnp.float32)
    ).astype(jnp.bfloat16)
    logits = jnp.dot(normed, router, preferred_element_type=jnp.float32)
    all_experts = jnp.arange(EXPERTS, dtype=jnp.int32)
    chosen = jnp.sum(jnp.where(routes[:, None] == all_experts[None, :], logits, 0.0), axis=1)
    gate_value = jax.nn.sigmoid(chosen)
    shared_hidden = jax.nn.gelu(
        jnp.dot(normed, shared_up, preferred_element_type=jnp.float32), approximate=True
    ).astype(jnp.bfloat16)
    total_tokens = routes.shape[0]
    capacity = 4 * total_tokens // EXPERTS
    column_count = expert_up.shape[1]
    local_units = min(column_count, FF)
    local_experts = column_count // local_units
    device_index = lax.axis_index("expert")
    first_expert = device_index * column_count // FF
    expert_ids = first_expert + jnp.arange(local_experts, dtype=jnp.int32)
    member = routes[:, None] == expert_ids[None, :]
    slot_rank = jnp.cumsum(member.astype(jnp.int32), axis=0) - 1
    slot_ids = jnp.arange(capacity, dtype=jnp.int32)
    placed = member[:, :, None] & (slot_rank[:, :, None] == slot_ids[None, None, :])
    picked = jnp.einsum(
        "skc,sd->kcd", placed.astype(jnp.bfloat16), normed, preferred_element_type=jnp.float32
    ).astype(jnp.bfloat16)
    up_local = expert_up.reshape(D, local_experts, local_units)
    inner_act = jax.nn.gelu(
        jnp.einsum("kcd,dkf->kcf", picked, up_local, preferred_element_type=jnp.float32),
        approximate=True,
    ).astype(jnp.bfloat16)
    down_local = expert_down.reshape(local_experts, local_units, D)
    result = jnp.einsum("kcf,kfd->kcd", inner_act, down_local, preferred_element_type=jnp.float32)
    spread = placed.astype(jnp.float32) * gate_value[:, None, None]
    summed = lax.psum_scatter(
        jnp.dot(shared_hidden, shared_down, preferred_element_type=jnp.float32)
        + jnp.einsum("skc,kcd->sd", spread, result, precision=lax.Precision.HIGHEST),
        "expert",
        scatter_dimension=0,
        tiled=True,
    )
    own_residual = lax.dynamic_slice_in_dim(residual, device_index * seq_count, seq_count, 0)
    combined = own_residual + summed
    return combined.astype(jnp.bfloat16)


def solution(mesh):
    placed = (
        P(("group", "expert"), None),
        P(("group", "expert"), None),
        P(("group", "expert"), None),
        P(("group", "expert"), None, None),
        P(("group", "expert"), None, None),
        P(("group", "expert")),
        P(("group", "expert"), None),
        P("group"),
        P(None, "expert"),
        P(),
        P(),
        P(None, "expert"),
        P("expert", None),
        P(None, "expert"),
        P("expert", None),
    )
    return jax.shard_map(
        body, mesh=mesh, in_specs=placed, out_specs=P(("group", "expert"), None), check_vma=False
    )
```

profile of v0, /device:TPU:0, one launch (start us, length us, event | category | flops | bytes accessed | tf_op | source)
XLA Modules:
  0.0 202.5 jit_solution(5360927554412156418)
XLA Ops:
  6.5 0.0 copy-start
  6.5 0.0 all-reduce.3.cloned.1.call-start
  6.5 1.6 copy.43
  8.8 0.9 fusion.42
  9.8 0.7 reduce.5
  10.5 0.7 reduce.6
  11.2 0.1 fusion.39
  11.4 0.1 fusion.41
  11.5 0.2 fusion.38
  11.7 0.1 fusion.44
  11.8 1.5 copy.47
  13.2 0.7 convert_element_type.86
  13.9 0.3 fusion.4
  14.3 0.1 add_convert_fusion
  14.4 23.5 %all-gather.1 = bf16[16,1,2048]{2,1,0:T(2,128)(2,1)S(1)} all-gather(bf16[1,1,2048]{2,1,0:T(2,128)(2,1)S(1)} %reshape.187), channel_id=1, replica_groups=mesh['group'=2,'expert'=16] {'expert'}, dimensions={0}, use_global_device_ids=true | all-gather | bytes 69632 | tf_op jit(solution)/shard_map/all_gather | solution.py:72
  37.8 1.2 convolution_convert_fusion.1
  39.1 17.6 %all_gather.11 = bf16[16,2048]{1,0:T(8,128)(2,1)S(1)} all-gather(bf16[16,128]{1,0:T(8,128)(2,1)S(1)} %convolution_convert_fusion.1), channel_id=1, replica_groups=mesh['group'=2,'expert'=16] {'expert'}, dimensions={1}, use_global_device_ids=true | all-gather | bytes 69632 | tf_op jit(solution)/shard_map/all_gather | solution.py:78
  56.7 19.3 %all-gather = bf16[16,1,2048]{2,1,0:T(2,128)(2,1)S(1)} all-gather(bf16[1,1,2048]{2,1,0:T(2,128)(2,1)} %bitcast.69), channel_id=1, replica_groups=mesh['group'=2,'expert'=16] {'expert'}, dimensions={0}, use_global_device_ids=true | all-gather | bytes 69632 | tf_op jit(solution)/shard_map/all_gather | solution.py:73
  76.0 0.2 fusion.57
  76.2 0.2 multiply_reduce_fusion
  76.4 0.7 convert_element_type.79
  77.1 0.7 fusion.56
  77.9 0.1 copy.30
  77.9 0.1 copy.29
  78.0 0.1 multiply_convert_fusion
  78.1 1.2 fusion.3
  79.3 12.2 %fusion.15 = bf16[2,2,4096]{2,1,0:T(2,128)(2,1)S(1)} fusion(bf16[256,2,8,4096]{3,2,1,0:T(8,128)(2,1)} %bitcast.63, bf16[16,2048]{1,0:T(8,128)(2,1)S(1)} %multiply_convert_fusion, pred[16,2,2]{0,1,2:T(4,128)(4,1)S(1)} %compare_and_fusion), kind=kOutput, calls=%fused_computation.22 | convolution fusion | flops 67526656 | bytes 33652800 | tf_op jit(solution)/shard_map/kcd,dkf->kcf/dot_general | solution.py:109
  91.5 0.0 copy-start.1
  91.5 12.8 %fusion.60 = f32[2,2,2048]{2,1,0:T(2,128)S(1)} fusion(bf16[2,2,4096]{2,1,0:T(2,128)(2,1)S(1)} %fusion.15, bf16[2,4096,2048]{2,1,0:T(8,128)(2,1)} %bitcast.64), kind=kOutput, calls=%fused_computation.80 | convolution fusion | flops 67108864 | bytes 33619968 | tf_op jit(solution)/shard_map/kcf,kfd->kcd/dot_general | solution.py:113
  104.4 0.4 convolution_bitcast_fusion
  104.7 0.0 copy-done
  104.8 3.0 %convolution_add_fusion = f32[16,2048]{1,0:T(8,128)} fusion(f32[16,2048]{1,0:T(8,128)S(1)} %convolution_bitcast_fusion, bf16[512,2048]{1,0:T(8,128)(2,1)S(1)} %copy-done, bf16[16,2048]{1,0:T(8,128)(2,1)S(1)} %multiply_convert_fusion, bf16[2048,512]{1,0:T(8,128)(2,1)} %param.26), kind=kOutput, calls=%fused_computation.4 | convolution fusion | flops 67215360 | bytes 4521984 | tf_op jit(solution)/shard_map/dot_general | solution.py:116
  107.8 0.0 all-reduce.3.cloned.1.call-update
  107.8 0.0 copy-done.1
  107.8 0.6 dynamic-slice
  108.4 85.1 %all-reduce.3.cloned.1.call-done = f32[16,2048]{1,0:T(8,128)} async-done(((f32[16,2048]{1,0:T(8,128)}), f32[16,2048]{1,0:T(8,128)}) %all-reduce.3.cloned.1.call-update) | async-done | bytes 131088
  193.5 2.1 %fusion.40 = bf16[1,2048]{1,0:T(2,128)(2,1)} fusion(f32[16,2048]{1,0:T(8,128)} %all-reduce.3.cloned.1.call-done, u32[]{:T(128)} %bitcast.14, f32[16,2048]{1,0:T(8,128)S(1)} %get-tuple-element.6, s32[]{:T(128)S(6)} %select_n.18), kind=kLoop, calls=%fused_computation.48 | loop fusion | flops 4096 | bytes 20488 | tf_op jit(solution)/shard_map/convert_element_type | solution.py:124
  (11 shorter events, 0.1 us)
Async XLA Ops:
  6.5 98.2 %copy-start = (bf16[512,2048]{1,0:T(8,128)(2,1)S(1)}, bf16[512,2048]{1,0:T(8,128)(2,1)}, u32[]{:S(2)}) copy-start(bf16[512,2048]{1,0:T(8,128)(2,1)} %param.27) | copy-start | bytes 6291460
  6.5 187.0 %all-reduce.3.cloned.1.call-start = ((), (), s32[]{:S(2)}) async-start(), calls=%async_computation | async-start | bytes 262144
  91.5 16.3 %copy-start.1 = (u32[32]{0:T(128)S(1)}, u32[32]{0:T(128)}, u32[]{:S(2)}) copy-start(u32[32]{0:T(128)} %constant.69) | copy-start | bytes 388
Sparse Core Ops, SparseCore 0:
  107.9 85.5 all-reduce.2
where the time goes:
time: 204 us; the launch traced here: 202 us
  waiting for transfers between devices  85.1 us (42%)
  blocking collectives  60.4 us (30%)
  matrix products  32 us (16%)
  between operations  14.2 us (7%)
  other arithmetic  6.8 us (3%)
  local copies, waits for them, and re-layouts  3.92 us (2%)
    unnamed x2, waiting for transfers between devices  85.1 us
    all_gather x1, blocking collectives, body(): lax.all_gather(attended, 'expert', axis=0, tiled=True)  23.5 us
    all_gather x1, blocking collectives, body(): lax.all_gather(hidden, 'expert', axis=0, tiled=True)  19.3 us
    all_gather x1, blocking collectives, body(): every_projected = lax.all_gather(projected, 'expert', axis=1, tiled=True)  17.6 us
    dot_general x1, matrix products, body(): jnp.einsum('kcf,kfd->kcd', inner_act, down_local, preferred_element_type=...  12.8 us
    dot_general x1, matrix products, body(): jnp.einsum('kcd,dkf->kcf', picked, up_local, preferred_element_type=jnp.f...  12.2 us
  transfers between devices with their start and end apart: 1, of which 1 were waited for; matrix products, arithmetic and copies ran while one was open for 0% of the time, Pallas kernels for 0%

commit v1 on v0

--- a/solution.py
+++ b/solution.py
@@ -1,8 +1,11 @@
+import functools
 import math
 
 import jax
 import jax.numpy as jnp
 from jax import lax
+from jax.experimental import pallas as pl
+from jax.experimental.pallas import tpu as pltpu
 from jax.sharding import PartitionSpec as P
 
 D = 2048
@@ -124,6 +127,314 @@
     return combined.astype(jnp.bfloat16)
 
 
+LANES = 128
+
+
+def per_head(row, heads):
+    index = lax.broadcasted_iota(jnp.int32, (heads, LANES), 0)
+    out = jnp.zeros((heads, LANES), jnp.float32)
+    for head in range(heads):
+        piece = row[:, head * LANES : (head + 1) * LANES]
+        out = jnp.where(index == head, piece, out)
+    return out
+
+
+def attend_kernel(
+    lengths, query, key_new, value_new, keys, values, hidden, out,
+    query_buf, key_new_buf, value_new_buf, hidden_buf, keys_buf, values_buf, sems,
+):
+    copies = [
+        pltpu.make_async_copy(source, target, sems.at[slot])
+        for slot, (source, target) in enumerate(
+            (
+                (query, query_buf),
+                (keys.at[0], keys_buf),
+                (key_new, key_new_buf),
+                (values.at[0], values_buf),
+                (value_new, value_new_buf),
+                (hidden, hidden_buf),
+            )
+        )
+    ]
+    for copy in copies:
+        copy.start()
+    cache_len, width = keys_buf.shape
+    heads = width // HEAD_DIM
+    scale_factor = 1.0 / math.sqrt(HEAD_DIM)
+    valid = lengths[0]
+    copies[0].wait()
+    lane_head = lax.broadcasted_iota(jnp.int32, (heads, width), 1) // HEAD_DIM
+    row_head = lax.broadcasted_iota(jnp.int32, (heads, width), 0)
+    head_query = jnp.where(lane_head == row_head, query_buf[...].astype(jnp.float32), 0.0)
+    copies[2].wait()
+    own_score = (
+        jnp.sum(head_query * key_new_buf[...].astype(jnp.float32), axis=1, keepdims=True)
+        * scale_factor
+    )
+    copies[1].wait()
+    scores = (
+        lax.dot_general(
+            head_query.astype(jnp.bfloat16),
+            keys_buf[...],
+            (((1,), (1,)), ((), ())),
+            preferred_element_type=jnp.float32,
+        )
+        * scale_factor
+    )
+    positions = lax.broadcasted_iota(jnp.int32, (heads, cache_len), 1)
+    scores = jnp.where(positions < valid, scores, -1e30)
+    top_score = jnp.maximum(jnp.max(scores, axis=1, keepdims=True), own_score)
+    weights = jnp.exp(scores - top_score)
+    own_weight = jnp.exp(own_score - top_score)
+    normalizer = jnp.sum(weights, axis=1, keepdims=True) + own_weight
+    weights = (weights / normalizer).astype(jnp.bfloat16)
+    own_weight = (own_weight / normalizer).astype(jnp.bfloat16).astype(jnp.float32)
+    copies[3].wait()
+    mixed = jnp.dot(weights, values_buf[...], preferred_element_type=jnp.float32)
+    copies[4].wait()
+    copies[5].wait()
+    own_value = per_head(value_new_buf[...].astype(jnp.float32), heads)
+    attended = (per_head(mixed, heads) + own_weight * own_value).astype(jnp.bfloat16)
+    residual = per_head(hidden_buf[...].astype(jnp.float32), heads).astype(jnp.bfloat16)
+    message = jnp.concatenate([attended, residual], axis=0)
+    out[...] = jnp.broadcast_to(message[None], out.shape)
+
+
+def project_kernel(gathered, w_out, out, hidden_out):
+    tokens, rows, _ = gathered.shape
+    total = tokens * rows
+    flat = gathered[...].reshape(total, LANES)
+    target = lax.broadcasted_iota(jnp.int32, (total, total), 0)
+    source = lax.broadcasted_iota(jnp.int32, (total, total), 1)
+    wanted = (target % tokens) * rows + target // tokens
+    swap = jnp.where(source == wanted, 1.0, 0.0).astype(jnp.bfloat16)
+    swapped = jnp.dot(swap, flat, preferred_element_type=jnp.float32).astype(jnp.bfloat16)
+    blocks = [swapped[row * tokens : (row + 1) * tokens] for row in range(rows)]
+    attended = jnp.concatenate(blocks[: rows // 2], axis=1)
+    hidden_out[...] = jnp.concatenate(blocks[rows // 2 :], axis=1)
+    projected = jnp.dot(attended, w_out[...], preferred_element_type=jnp.float32)
+    out[...] = jnp.broadcast_to(projected.astype(jnp.bfloat16)[None], out.shape)
+
+
+def gelu(value):
+    return jax.nn.gelu(value, approximate=True).astype(jnp.bfloat16)
+
+
+def mlp_kernel(
+    axis, local_experts, up_step, down_step, slots,
+    routes, projected, hidden, ln_gain, router, shared_up, shared_down, expert_up, expert_down,
+    out, own_out,
+    router_buf, shared_up_buf, shared_down_buf, down_buf, act_buf, sems, down_sems,
+):
+    device_index = lax.axis_index(axis)
+    tokens, width = hidden.shape
+    columns = expert_up.shape[1]
+    units = columns // local_experts
+    down_count = columns // down_step
+
+    def down_copy(index):
+        slot = lax.rem(index, slots)
+        return pltpu.make_async_copy(
+            expert_down.at[pl.ds(pl.multiple_of(index * down_step, down_step), down_step)],
+            down_buf.at[slot],
+            down_sems.at[slot],
+        )
+
+    router_copy = pltpu.make_async_copy(router, router_buf, sems.at[0])
+    shared_up_copy = pltpu.make_async_copy(shared_up, shared_up_buf, sems.at[1])
+    shared_down_copy = pltpu.make_async_copy(shared_down, shared_down_buf, sems.at[2])
+    shared_up_copy.start()
+    router_copy.start()
+    shared_down_copy.start()
+    for index in range(min(slots, down_count)):
+        down_copy(index).start()
+
+    blocks = width // LANES
+    every_projected = jnp.concatenate(
+        [projected[block].astype(jnp.float32) for block in range(projected.shape[0])], axis=1
+    )
+    residual = hidden[...].astype(jnp.float32) + every_projected
+    token = lax.broadcasted_iota(jnp.int32, (tokens, width), 0)
+    own = jnp.sum(jnp.where(token == device_index, residual, 0.0), axis=0, keepdims=True)
+    own_out[...] = per_head(own, blocks)
+    centered = residual - jnp.mean(residual, axis=1, keepdims=True)
+    variance = jnp.mean(centered * centered, axis=1, keepdims=True)
+    gain = ln_gain[...].astype(jnp.float32)
+    gain = jnp.concatenate([gain[block : block + 1] for block in range(blocks)], axis=1)
+    normed = (centered / jnp.sqrt(jnp.maximum(variance, 0.25)) * gain).astype(jnp.bfloat16)
+
+    def up_body(step, carry):
+        at = pl.ds(pl.multiple_of(step * up_step, up_step), up_step)
+        act_buf[:, at] = gelu(
+            jnp.dot(normed, expert_up[:, at], preferred_element_type=jnp.float32)
+        )
+        return carry
+
+    lax.fori_loop(0, columns // up_step, up_body, 0)
+
+    router_copy.wait()
+    logits = lax.dot_general(
+        normed, router_buf[...], (((1,), (1,)), ((), ())), preferred_element_type=jnp.float32
+    )
+    experts = logits.shape[1]
+    token_column = lax.broadcasted_iota(jnp.int32, (tokens, 1), 0)
+    route = jnp.zeros((tokens, 1), jnp.int32)
+    for index in range(tokens):
+        route = jnp.where(token_column == index, routes[index], route)
+    expert_lane = lax.broadcasted_iota(jnp.int32, (tokens, experts), 1)
+    chosen = jnp.sum(jnp.where(expert_lane == route, logits, 0.0), axis=1, keepdims=True)
+    gate = jax.nn.sigmoid(chosen)
+    shared_up_copy.wait()
+    shared_act = gelu(jnp.dot(normed, shared_up_buf[...], preferred_element_type=jnp.float32))
+    shared_down_copy.wait()
+    total = jnp.dot(shared_act, shared_down_buf[...], preferred_element_type=jnp.float32)
+
+    for expert in range(local_experts):
+        first = expert * (units // down_step)
+
+        def down_body(step, sums):
+            index = first + step
+            slot = lax.rem(index, slots)
+            down_copy(index).wait()
+            at = pl.ds(pl.multiple_of(index * down_step, down_step), down_step)
+            sums = sums + jnp.dot(
+                act_buf[:, at], down_buf[slot], preferred_element_type=jnp.float32
+            )
+
+            @pl.when(index + slots < down_count)
+            def _():
+                down_copy(index + slots).start()
+
+            return sums
+
+        sums = lax.fori_loop(
+            0, units // down_step, down_body, jnp.zeros((tokens, width), jnp.float32)
+        )
+        here = route == device_index * local_experts + expert
+        total = total + jnp.where(here, gate, 0.0) * sums
+
+    for block in range(blocks):
+        out[:, block, :] = total[:, block * LANES : (block + 1) * LANES]
+
+
+def combine_kernel(terms, own, out):
+    total = own[...]
+    for index in range(terms.shape[0]):
+        total = total + terms[index]
+    for block in range(total.shape[0]):
+        out[:, block * LANES : (block + 1) * LANES] = total[block : block + 1].astype(out.dtype)
+
+
+VMEM = pl.BlockSpec(memory_space=pltpu.VMEM)
+SMEM = pl.BlockSpec(memory_space=pltpu.SMEM)
+HBM = pl.BlockSpec(memory_space=pltpu.HBM)
+
+
+def params(megabytes):
+    return pltpu.CompilerParams(vmem_limit_bytes=megabytes << 20)
+
+
+def cost(flops):
+    return pl.CostEstimate(flops=flops, bytes_accessed=flops >> 8, transcendentals=0)
+
+
+def fast_body(
+    query, key_new, value_new, key_cache, value_cache, lengths, hidden, routes, w_out,
+    ln_gain, router, shared_up, shared_down, expert_up, expert_down,
+):
+    width = query.shape[1]
+    blocks = width // LANES
+    cache_len = key_cache.shape[1]
+    tokens = routes.shape[0]
+    columns = expert_up.shape[1]
+    in_hbm = functools.partial(pltpu.with_memory_space_constraint, memory_space=pltpu.HBM)
+    query, key_new, value_new, key_cache, value_cache, hidden = map(
+        in_hbm, (query, key_new, value_new, key_cache, value_cache, hidden)
+    )
+    router, shared_up, shared_down, expert_down = map(
+        in_hbm, (router.T, shared_up, shared_down, expert_down)
+    )
+    expert_up = pltpu.with_memory_space_constraint(expert_up, pltpu.VMEM)
+    row = pltpu.VMEM((1, width), jnp.bfloat16)
+    cache = pltpu.VMEM((cache_len, width), jnp.bfloat16)
+    message = pl.pallas_call(
+        attend_kernel,
+        out_shape=jax.ShapeDtypeStruct((tokens, 2 * blocks, LANES), jnp.bfloat16),
+        in_specs=[SMEM] + [HBM] * 6,
+        out_specs=VMEM,
+        scratch_shapes=[row] * 4 + [cache] * 2 + [pltpu.SemaphoreType.DMA((6,))],
+        compiler_params=params(4),
+        cost_estimate=cost(10**11),
+        name="attend",
+    )(lengths, query, key_new, value_new, key_cache, value_cache, hidden)
+    gathered = lax.all_to_all(message, "expert", 0, 0)
+    message, every_hidden = pl.pallas_call(
+        project_kernel,
+        out_shape=(
+            jax.ShapeDtypeStruct((tokens, tokens, LANES), jnp.bfloat16),
+            jax.ShapeDtypeStruct((tokens, width), jnp.bfloat16),
+        ),
+        in_specs=[VMEM] * 2,
+        out_specs=(VMEM, VMEM),
+        compiler_params=params(4),
+        cost_estimate=cost(10**11),
+        name="project",
+    )(gathered, w_out)
+    every_projected = lax.all_to_all(message, "expert", 0, 0)
+    local_experts = columns // FF
+    slots, down_step, up_step = 11, 512, 1024
+    terms, own = pl.pallas_call(
+        functools.partial(mlp_kernel, "expert", local_experts, up_step, down_step, slots),
+        out_shape=(
+            jax.ShapeDtypeStruct((tokens, blocks, LANES), jnp.float32),
+            jax.ShapeDtypeStruct((blocks, LANES), jnp.float32),
+        ),
+        in_specs=[SMEM, VMEM, VMEM, VMEM, HBM, HBM, HBM, VMEM, HBM],
+        out_specs=(VMEM, VMEM),
+        scratch_shapes=[
+            pltpu.VMEM(router.shape, router.dtype),
+            pltpu.VMEM(shared_up.shape, shared_up.dtype),
+            pltpu.VMEM(shared_down.shape, shared_down.dtype),
+            pltpu.VMEM((slots, down_step, width), expert_down.dtype),
+            pltpu.VMEM((tokens, columns), jnp.bfloat16),
+            pltpu.SemaphoreType.DMA((3,)),
+            pltpu.SemaphoreType.DMA((slots,)),
+        ],
+        compiler_params=params(29),
+        cost_estimate=cost(10**11),
+        name="mlp",
+    )(
+        routes, every_projected, every_hidden, ln_gain.reshape(blocks, LANES), router,
+        shared_up, shared_down, expert_up, expert_down,
+    )
+    terms = lax.all_to_all(terms, "expert", 0, 0)
+    return pl.pallas_call(
+        combine_kernel,
+        out_shape=jax.ShapeDtypeStruct((1, width), jnp.bfloat16),
+        in_specs=[VMEM] * 2,
+        out_specs=VMEM,
+        compiler_params=params(2),
+        name="combine",
+    )(terms, own)
+
+
+def fits_fast(
+    query, key_new, value_new, key_cache, value_cache, lengths, hidden, routes, w_out, *rest
+):
+    tokens = routes.shape[0]
+    return (
+        query.shape[0] == 1
+        and HEAD_DIM == LANES
+        and w_out.shape[1] == LANES
+        and tokens * LANES == query.shape[1]
+        and rest[4].shape[1] % FF == 0
+    )
+
+
+def pick_body(*args):
+    return fast_body(*args) if fits_fast(*args) else body(*args)
+
+
 def solution(mesh):
     placed = (
         P(("group", "expert"), None),
@@ -143,5 +454,5 @@
         P("expert", None),
     )
     return jax.shard_map(
-        body, mesh=mesh, in_specs=placed, out_specs=P(("group", "expert"), None), check_vma=False
-    )
+        pick_body, mesh=mesh, in_specs=placed, out_specs=P(("group", "expert"), None), check_vma=False
+    )

time: 204 us -> 59.3 us (0.29)
  waiting for transfers between devices: 85.1 us -> 0 us
  matrix products: 32 us -> 0 us
  blocking collectives: 60.4 us -> 37.2 us
  Pallas kernels: 0 us -> 20.4 us
  between operations: 14.2 us -> 0.69 us
  other arithmetic: 6.8 us -> 0 us
  local copies, waits for them, and re-layouts: 3.92 us -> 0.71 us
    unnamed x2 -> x0, waiting for transfers between devices: 85.1 us -> none
    all_gather x3 -> x0, blocking collectives: 60.4 us -> none  [the longest x1 23.5 us: body(): lax.all_gather(attended, 'expert', axis=0, tiled=True)]
    all_to_all x0 -> x3, blocking collectives: none -> 37.2 us  [the longest x1 15.1 us: fast_body(): gathered = lax.all_to_all(message, 'expert', 0, 0)]
    dot_general x8 -> x0, matrix products: 32 us -> none  [the longest x1 12.8 us: body(): jnp.einsum('kcf,kfd->kcd', inner_act, down_local, preferred_element_type=...]
    pallas_call x0 -> x4, Pallas kernels: none -> 20.4 us  [the longest x1 16.8 us: fast_body(): pl.pallas_call(functools.partial(mlp_kernel, 'expert', local_experts, up_...]
    convert_element_type x8 -> x0, other arithmetic: 4.48 us -> none  [the longest x1 2.08 us: body(): return combined.astype(jnp.bfloat16)]
  transfers between devices with their start and end apart: 1 -> 0, of which waited for: 1 -> 0; matrix products, arithmetic and copies ran while one was open for 0% -> 0% of each run, Pallas kernels for 0% -> 0%
where the time goes in v1:
time: 59.3 us; the launch traced here: 59 us
  blocking collectives  37.2 us (63%)
  Pallas kernels  20.4 us (34%)
  local copies, waits for them, and re-layouts  0.71 us (1%)
  between operations  0.69 us (1%)
    pallas_call x1, Pallas kernels, fast_body(): pl.pallas_call(functools.partial(mlp_kernel, 'expert', local_experts, up_...  16.8 us
    all_to_all x1, blocking collectives, fast_body(): gathered = lax.all_to_all(message, 'expert', 0, 0)  15.1 us
    all_to_all x1, blocking collectives, fast_body(): terms = lax.all_to_all(terms, 'expert', 0, 0)  11.4 us
    all_to_all x1, blocking collectives, fast_body(): every_projected = lax.all_to_all(message, 'expert', 0, 0)  10.7 us
    pallas_call x1, Pallas kernels, fast_body(): pl.pallas_call(attend_kernel, out_shape=jax.ShapeDtypeStruct((tokens, 2 *...  2.47 us

profile of v1, /device:TPU:0, one launch (start us, length us, event | category | flops | bytes accessed | tf_op | source)
XLA Modules:
  0.0 59.0 jit_solution(7498503198312984122)
XLA Ops:
  0.7 0.0 copy-start.2
  0.7 2.5 %attend.1 = bf16[16,32,128]{2,1,0:T(8,128)(2,1)S(1)} custom-call(s32[1]{0:T(128)S(6)} %copy.16.lengths, bf16[1,2048]{1,0:T(2,128)(2,1)} %query.1, bf16[1,2048]{1,0:T(2,128)(2,1)} %key_new.1, bf16[1,2048]{1,0:T(2,128)(2,1)} %value_new.1, bf16[1,256,2048]{2,1,0:T(8,128)(2,1)} %keys.1, bf16[1,256,2048]{2,1,0:T(8,128)(2,1)} %values.1, bf16[1,2048]{1,0:T(2,128)(2,1)} %hidden.1), custom_call_target="tpu_custom_call" | custom-call | flops 99999997952 | bytes 390624992 | tf_op jit(solution)/shard_map/attend/pallas_call | solution.py:360
  3.1 15.1 %all_to_all.15.gathered = bf16[16,32,128]{2,1,0:T(8,128)(2,1)S(1)} all-to-all(bf16[16,32,128]{2,1,0:T(8,128)(2,1)S(1)} %attend.1), channel_id=1, replica_groups=mesh['group'=2,'expert'=16] {'expert'}, dimensions={0} | all-to-all | bytes 262144 | tf_op jit(solution)/shard_map/all_to_all | solution.py:370
  18.3 0.0 copy-done.2
  18.3 0.0 copy-start.1
  18.3 0.5 project.1
  18.7 0.0 copy-start.3
  18.7 10.7 %all_to_all.16.projected = bf16[16,16,128]{2,1,0:T(8,128)(2,1)} all-to-all(bf16[16,16,128]{2,1,0:T(8,128)(2,1)S(1)} %get-tuple-element.9), channel_id=1, replica_groups=mesh['group'=2,'expert'=16] {'expert'}, dimensions={0} | all-to-all | bytes 131072 | tf_op jit(solution)/shard_map/all_to_all | solution.py:383
  29.4 0.0 copy-done.3
  29.4 0.0 copy-done.1
  29.4 16.8 %mlp.1 = (f32[16,16,128]{2,1,0:T(8,128)}, f32[16,128]{1,0:T(8,128)}) custom-call(s32[16]{0:T(128)} %routes.1, bf16[16,16,128]{2,1,0:T(8,128)(2,1)} %all_to_all.16.projected, bf16[16,2048]{1,0:T(8,128)(2,1)} %copy-done.3, bf16[16,128]{1,0:T(8,128)(2,1)} %bitcast.3, bf16[32,2048]{1,0:T(8,128)(2,1)} %bitcast.2, bf16[2048,512]{1,0:T(8,128)(2,1)} %shared_up.1, ...), custom_call_target="tpu_custom_call" | custom-call | flops 99999997952 | bytes 390624992 | tf_op jit(solution)/shard_map/mlp/pallas_call | solution.py:386
  46.2 11.4 %all_to_all.17.terms = f32[16,16,128]{2,1,0:T(8,128)S(1)} all-to-all(f32[16,16,128]{2,1,0:T(8,128)} %get-tuple-element.11), channel_id=1, replica_groups=mesh['group'=2,'expert'=16] {'expert'}, dimensions={0} | all-to-all | bytes 262144 | tf_op jit(solution)/shard_map/all_to_all | solution.py:410
  57.6 0.0 copy-start
  57.6 0.7 %copy-done = f32[16,128]{1,0:T(8,128)S(1)} copy-done((f32[16,128]{1,0:T(8,128)S(1)}, f32[16,128]{1,0:T(8,128)}, u32[]{:S(2)}) %copy-start) | copy-done | bytes 8216
  58.3 0.6 %combine.1 = bf16[1,2048]{1,0:T(2,128)(2,1)} custom-call(f32[16,16,128]{2,1,0:T(8,128)S(1)} %all_to_all.17.terms, f32[16,128]{1,0:T(8,128)S(1)} %copy-done), custom_call_target="tpu_custom_call" | custom-call | tf_op jit(solution)/shard_map/combine/pallas_call | solution.py:411
Async XLA Ops:
  0.7 17.6 %copy-start.2 = (bf16[2048,128]{1,0:T(8,128)(2,1)S(1)}, bf16[2048,128]{1,0:T(8,128)(2,1)}, u32[]{:S(2)}) copy-start(bf16[2048,128]{1,0:T(8,128)(2,1)} %w_out.1) | copy-start | bytes 1572868
  18.3 11.2 %copy-start.1 = (bf16[2048,8192]{1,0:T(8,128)(2,1)S(1)}, bf16[2048,8192]{1,0:T(8,128)(2,1)}, u32[]{:S(2)}) copy-start(bf16[2048,8192]{1,0:T(8,128)(2,1)} %expert_up.1) | copy-start | bytes 100663296
  18.7 10.7 %copy-start.3 = (bf16[16,2048]{1,0:T(8,128)(2,1)}, bf16[16,2048]{1,0:T(8,128)(2,1)S(1)}, u32[]{:S(2)}) copy-start(bf16[16,2048]{1,0:T(8,128)(2,1)S(1)} %get-tuple-element.10.hidden) | copy-start | bytes 196612
  57.6 0.7 %copy-start = (f32[16,128]{1,0:T(8,128)S(1)}, f32[16,128]{1,0:T(8,128)}, u32[]{:S(2)}) copy-start(f32[16,128]{1,0:T(8,128)} %get-tuple-element.12.own) | copy-start | bytes 24580

commit v2 on v1

--- a/solution.py
+++ b/solution.py
@@ -200,7 +200,7 @@
     out[...] = jnp.broadcast_to(message[None], out.shape)
 
 
-def project_kernel(gathered, w_out, out, hidden_out):
+def project_kernel(gathered, w_out, shared_up, shared_down, out, hidden_out):
     tokens, rows, _ = gathered.shape
     total = tokens * rows
     flat = gathered[...].reshape(total, LANES)
@@ -224,7 +224,7 @@
     axis, local_experts, up_step, down_step, slots,
     routes, projected, hidden, ln_gain, router, shared_up, shared_down, expert_up, expert_down,
     out, own_out,
-    router_buf, shared_up_buf, shared_down_buf, down_buf, act_buf, sems, down_sems,
+    router_buf, down_buf, act_buf, router_sem, down_sems,
 ):
     device_index = lax.axis_index(axis)
     tokens, width = hidden.shape
@@ -233,19 +233,15 @@
     down_count = columns // down_step
 
     def down_copy(index):
-        slot = lax.rem(index, slots)
+        slot = index % slots
         return pltpu.make_async_copy(
-            expert_down.at[pl.ds(pl.multiple_of(index * down_step, down_step), down_step)],
+            expert_down.at[index * down_step : (index + 1) * down_step],
             down_buf.at[slot],
             down_sems.at[slot],
         )
 
-    router_copy = pltpu.make_async_copy(router, router_buf, sems.at[0])
-    shared_up_copy = pltpu.make_async_copy(shared_up, shared_up_buf, sems.at[1])
-    shared_down_copy = pltpu.make_async_copy(shared_down, shared_down_buf, sems.at[2])
-    shared_up_copy.start()
+    router_copy = pltpu.make_async_copy(router, router_buf, router_sem)
     router_copy.start()
-    shared_down_copy.start()
     for index in range(min(slots, down_count)):
         down_copy(index).start()
 
@@ -263,15 +259,6 @@
     gain = jnp.concatenate([gain[block : block + 1] for block in range(blocks)], axis=1)
     normed = (centered / jnp.sqrt(jnp.maximum(variance, 0.25)) * gain).astype(jnp.bfloat16)
 
-    def up_body(step, carry):
-        at = pl.ds(pl.multiple_of(step * up_step, up_step), up_step)
-        act_buf[:, at] = gelu(
-            jnp.dot(normed, expert_up[:, at], preferred_element_type=jnp.float32)
-        )
-        return carry
-
-    lax.fori_loop(0, columns // up_step, up_body, 0)
-
     router_copy.wait()
     logits = lax.dot_general(
         normed, router_buf[...], (((1,), (1,)), ((), ())), preferred_element_type=jnp.float32
@@ -284,32 +271,26 @@
     expert_lane = lax.broadcasted_iota(jnp.int32, (tokens, experts), 1)
     chosen = jnp.sum(jnp.where(expert_lane == route, logits, 0.0), axis=1, keepdims=True)
     gate = jax.nn.sigmoid(chosen)
-    shared_up_copy.wait()
-    shared_act = gelu(jnp.dot(normed, shared_up_buf[...], preferred_element_type=jnp.float32))
-    shared_down_copy.wait()
-    total = jnp.dot(shared_act, shared_down_buf[...], preferred_element_type=jnp.float32)
+    shared_act = gelu(jnp.dot(normed, shared_up[...], preferred_element_type=jnp.float32))
+    total = jnp.dot(shared_act, shared_down[...], preferred_element_type=jnp.float32)
 
     for expert in range(local_experts):
         first = expert * (units // down_step)
 
-        def down_body(step, sums):
-            index = first + step
-            slot = lax.rem(index, slots)
+        for step in range(expert * units // up_step, (expert + 1) * units // up_step):
+            at = slice(step * up_step, (step + 1) * up_step)
+            act_buf[:, at] = gelu(
+                jnp.dot(normed, expert_up[:, at], preferred_element_type=jnp.float32)
+            )
+        sums = jnp.zeros((tokens, width), jnp.float32)
+        for index in range(first, first + units // down_step):
             down_copy(index).wait()
-            at = pl.ds(pl.multiple_of(index * down_step, down_step), down_step)
+            at = slice(index * down_step, (index + 1) * down_step)
             sums = sums + jnp.dot(
-                act_buf[:, at], down_buf[slot], preferred_element_type=jnp.float32
+                act_buf[:, at], down_buf[index % slots], preferred_element_type=jnp.float32
             )
-
-            @pl.when(index + slots < down_count)
-            def _():
+            if index + slots < down_count:
                 down_copy(index + slots).start()
-
-            return sums
-
-        sums = lax.fori_loop(
-            0, units // down_step, down_body, jnp.zeros((tokens, width), jnp.float32)
-        )
         here = route == device_index * local_experts + expert
         total = total + jnp.where(here, gate, 0.0) * sums
 
@@ -338,6 +319,37 @@
     return pl.CostEstimate(flops=flops, bytes_accessed=flops >> 8, transcendentals=0)
 
 
+def mlp(
+    routes, projected, hidden, ln_gain, router, shared_up, shared_down, expert_up, expert_down
+):
+    tokens, width = hidden.shape
+    blocks = width // LANES
+    columns = expert_up.shape[1]
+    local_experts = columns // FF
+    slots, down_step, up_step = 9, 512, 1024
+    return pl.pallas_call(
+        functools.partial(mlp_kernel, "expert", local_experts, up_step, down_step, slots),
+        out_shape=(
+            pltpu.VMEM((tokens, blocks, LANES), jnp.float32),
+            pltpu.VMEM((blocks, LANES), jnp.float32),
+        ),
+        in_specs=[SMEM, VMEM, VMEM, VMEM, HBM, VMEM, VMEM, VMEM, HBM],
+        out_specs=(VMEM, VMEM),
+        scratch_shapes=[
+            pltpu.VMEM(router.shape, router.dtype),
+            pltpu.VMEM((slots, down_step, width), expert_down.dtype),
+            pltpu.VMEM((tokens, columns), jnp.bfloat16),
+            pltpu.SemaphoreType.DMA,
+            pltpu.SemaphoreType.DMA((slots,)),
+        ],
+        compiler_params=params(25),
+        cost_estimate=cost(10**11),
+        name="mlp",
+    )(
+        routes, projected, hidden, ln_gain, router, shared_up, shared_down, expert_up, expert_down
+    )
+
+
 def fast_body(
     query, key_new, value_new, key_cache, value_cache, lengths, hidden, routes, w_out,
     ln_gain, router, shared_up, shared_down, expert_up, expert_down,
@@ -346,15 +358,13 @@
     blocks = width // LANES
     cache_len = key_cache.shape[1]
     tokens = routes.shape[0]
-    columns = expert_up.shape[1]
     in_hbm = functools.partial(pltpu.with_memory_space_constraint, memory_space=pltpu.HBM)
     query, key_new, value_new, key_cache, value_cache, hidden = map(
         in_hbm, (query, key_new, value_new, key_cache, value_cache, hidden)
     )
-    router, shared_up, shared_down, expert_down = map(
-        in_hbm, (router.T, shared_up, shared_down, expert_down)
-    )
-    expert_up = pltpu.with_memory_space_constraint(expert_up, pltpu.VMEM)
+    in_vmem = functools.partial(pltpu.with_memory_space_constraint, memory_space=pltpu.VMEM)
+    router, expert_down = map(in_hbm, (router.T, expert_down))
+    shared_up, shared_down, expert_up = map(in_vmem, (shared_up, shared_down, expert_up))
     row = pltpu.VMEM((1, width), jnp.bfloat16)
     cache = pltpu.VMEM((cache_len, width), jnp.bfloat16)
     message = pl.pallas_call(
@@ -374,37 +384,15 @@
             jax.ShapeDtypeStruct((tokens, tokens, LANES), jnp.bfloat16),
             jax.ShapeDtypeStruct((tokens, width), jnp.bfloat16),
         ),
-        in_specs=[VMEM] * 2,
+        in_specs=[VMEM] * 4,
         out_specs=(VMEM, VMEM),
         compiler_params=params(4),
         cost_estimate=cost(10**11),
         name="project",
-    )(gathered, w_out)
+    )(gathered, w_out, shared_up, shared_down)
     every_projected = lax.all_to_all(message, "expert", 0, 0)
-    local_experts = columns // FF
-    slots, down_step, up_step = 11, 512, 1024
-    terms, own = pl.pallas_call(
-        functools.partial(mlp_kernel, "expert", local_experts, up_step, down_step, slots),
-        out_shape=(
-            jax.ShapeDtypeStruct((tokens, blocks, LANES), jnp.float32),
-            jax.ShapeDtypeStruct((blocks, LANES), jnp.float32),
-        ),
-        in_specs=[SMEM, VMEM, VMEM, VMEM, HBM, HBM, HBM, VMEM, HBM],
-        out_specs=(VMEM, VMEM),
-        scratch_shapes=[
-            pltpu.VMEM(router.shape, router.dtype),
-            pltpu.VMEM(shared_up.shape, shared_up.dtype),
-            pltpu.VMEM(shared_down.shape, shared_down.dtype),
-            pltpu.VMEM((slots, down_step, width), expert_down.dtype),
-            pltpu.VMEM((tokens, columns), jnp.bfloat16),
-            pltpu.SemaphoreType.DMA((3,)),
-            pltpu.SemaphoreType.DMA((slots,)),
-        ],
-        compiler_params=params(29),
-        cost_estimate=cost(10**11),
-        name="mlp",
-    )(
-        routes, every_projected, every_hidden, ln_gain.reshape(blocks, LANES), router,
+    terms, own = mlp(
+        routes, in_vmem(every_projected), in_vmem(every_hidden), ln_gain.reshape(blocks, LANES), router,
         shared_up, shared_down, expert_up, expert_down,
     )
     terms = lax.all_to_all(terms, "expert", 0, 0)

time: 59.3 us -> 52.5 us (0.89)
  Pallas kernels: 20.4 us -> 15.7 us
  blocking collectives: 37.2 us -> 35.6 us
  local copies, waits for them, and re-layouts: 0.71 us -> 0.08 us
    pallas_call x1, Pallas kernels: 16.8 us -> 12.1 us  [mlp(): pl.pallas_call(functools.partial(mlp_kernel, 'expert', local_experts, up_...]
    all_to_all x1, blocking collectives: 11.4 us -> 10.5 us  [fast_body(): terms = lax.all_to_all(terms, 'expert', 0, 0)]
    all_to_all x1, blocking collectives: 10.7 us -> 10 us  [fast_body(): every_projected = lax.all_to_all(message, 'expert', 0, 0)]
    unnamed x8, local copies, waits for them, and re-layouts: 0.71 us -> 0.08 us
where the time goes in v2:
time: 52.5 us; the launch traced here: 52.2 us
  blocking collectives  35.6 us (68%)
  Pallas kernels  15.7 us (30%)
  between operations  0.71 us (1%)
    all_to_all x1, blocking collectives, fast_body(): gathered = lax.all_to_all(message, 'expert', 0, 0)  15.1 us
    pallas_call x1, Pallas kernels, mlp(): pl.pallas_call(functools.partial(mlp_kernel, 'expert', local_experts, up_...  12.1 us
    all_to_all x1, blocking collectives, fast_body(): terms = lax.all_to_all(terms, 'expert', 0, 0)  10.5 us
    all_to_all x1, blocking collectives, fast_body(): every_projected = lax.all_to_all(message, 'expert', 0, 0)  10 us
    pallas_call x1, Pallas kernels, fast_body(): pl.pallas_call(attend_kernel, out_shape=jax.ShapeDtypeStruct((tokens, 2 *...  2.56 us

profile of v2, /device:TPU:0, one launch (start us, length us, event | category | flops | bytes accessed | tf_op | source)
XLA Modules:
  0.0 52.2 jit_solution(17364639625595698094)
XLA Ops:
  0.7 0.0 copy-start.1
  0.7 0.0 copy-start.2
  0.7 0.0 copy-start.3
  0.7 2.6 %attend.1 = bf16[16,32,128]{2,1,0:T(8,128)(2,1)S(1)} custom-call(s32[1]{0:T(128)S(6)} %copy.16.lengths, bf16[1,2048]{1,0:T(2,128)(2,1)} %query.1, bf16[1,2048]{1,0:T(2,128)(2,1)} %key_new.1, bf16[1,2048]{1,0:T(2,128)(2,1)} %value_new.1, bf16[1,256,2048]{2,1,0:T(8,128)(2,1)} %keys.1, bf16[1,256,2048]{2,1,0:T(8,128)(2,1)} %values.1, bf16[1,2048]{1,0:T(2,128)(2,1)} %hidden.1), custom_call_target="tpu_custom_call" | custom-call | flops 99999997952 | bytes 390624992 | tf_op jit(solution)/shard_map/attend/pallas_call | solution.py:370
  3.2 15.1 %all_to_all.15.gathered = bf16[16,32,128]{2,1,0:T(8,128)(2,1)S(1)} all-to-all(bf16[16,32,128]{2,1,0:T(8,128)(2,1)S(1)} %attend.1), channel_id=1, replica_groups=mesh['group'=2,'expert'=16] {'expert'}, dimensions={0} | all-to-all | bytes 262144 | tf_op jit(solution)/shard_map/all_to_all | solution.py:380
  18.4 0.0 copy-done.1
  18.4 0.0 copy-done.2
  18.4 0.0 copy-done.3
  18.4 0.0 copy-start
  18.4 0.5 project.1
  18.9 10.0 %all_to_all.16.projected = bf16[16,16,128]{2,1,0:T(8,128)(2,1)S(1)} all-to-all(bf16[16,16,128]{2,1,0:T(8,128)(2,1)S(1)} %get-tuple-element.9), channel_id=1, replica_groups=mesh['group'=2,'expert'=16] {'expert'}, dimensions={0} | all-to-all | bytes 131072 | tf_op jit(solution)/shard_map/all_to_all | solution.py:393
  28.9 0.1 copy-done
  28.9 12.1 %mlp.1 = (f32[16,16,128]{2,1,0:T(8,128)S(1)}, f32[16,128]{1,0:T(8,128)S(1)}) custom-call(s32[16]{0:T(128)} %routes.1, bf16[16,16,128]{2,1,0:T(8,128)(2,1)S(1)} %all_to_all.16.projected, bf16[16,2048]{1,0:T(8,128)(2,1)S(1)} %get-tuple-element.10.hidden, bf16[16,128]{1,0:T(8,128)(2,1)} %bitcast.3, bf16[32,2048]{1,0:T(8,128)(2,1)} %bitcast.2, ...), custom_call_target="tpu_custom_call" | custom-call | flops 99999997952 | bytes 390624992 | tf_op jit(solution)/shard_map/mlp/pallas_call | solution.py:330
  41.0 10.5 %all_to_all.17.terms = f32[16,16,128]{2,1,0:T(8,128)S(1)} all-to-all(f32[16,16,128]{2,1,0:T(8,128)S(1)} %get-tuple-element.11), channel_id=1, replica_groups=mesh['group'=2,'expert'=16] {'expert'}, dimensions={0} | all-to-all | bytes 262144 | tf_op jit(solution)/shard_map/all_to_all | solution.py:398
  51.5 0.6 %combine.1 = bf16[1,2048]{1,0:T(2,128)(2,1)} custom-call(f32[16,16,128]{2,1,0:T(8,128)S(1)} %all_to_all.17.terms, f32[16,128]{1,0:T(8,128)S(1)} %get-tuple-element.12.own), custom_call_target="tpu_custom_call" | custom-call | tf_op jit(solution)/shard_map/combine/pallas_call | solution.py:399
Async XLA Ops:
  0.7 17.7 %copy-start.1 = (bf16[2048,512]{1,0:T(8,128)(2,1)S(1)}, bf16[2048,512]{1,0:T(8,128)(2,1)}, u32[]{:S(2)}) copy-start(bf16[2048,512]{1,0:T(8,128)(2,1)} %shared_up.3) | copy-start | bytes 6291460
  0.7 17.7 %copy-start.2 = (bf16[512,2048]{1,0:T(8,128)(2,1)S(1)}, bf16[512,2048]{1,0:T(8,128)(2,1)}, u32[]{:S(2)}) copy-start(bf16[512,2048]{1,0:T(8,128)(2,1)} %shared_down.3) | copy-start | bytes 6291460
  0.7 17.7 %copy-start.3 = (bf16[2048,128]{1,0:T(8,128)(2,1)S(1)}, bf16[2048,128]{1,0:T(8,128)(2,1)}, u32[]{:S(2)}) copy-start(bf16[2048,128]{1,0:T(8,128)(2,1)} %w_out.1) | copy-start | bytes 1572868
  18.4 10.5 %copy-start = (bf16[2048,8192]{1,0:T(8,128)(2,1)S(1)}, bf16[2048,8192]{1,0:T(8,128)(2,1)}, u32[]{:S(2)}) copy-start(bf16[2048,8192]{1,0:T(8,128)(2,1)} %expert_up.1) | copy-start | bytes 100663296

commit v3 on v2

--- a/solution.py
+++ b/solution.py
@@ -128,6 +128,7 @@
 
 
 LANES = 128
+HEAD_ROWS = 1024
 
 
 def per_head(row, heads):
@@ -140,9 +141,11 @@
 
 
 def attend_kernel(
-    lengths, query, key_new, value_new, keys, values, hidden, out,
+    axis, lengths, query, key_new, value_new, keys, values, hidden, expert_down, out, down_head,
     query_buf, key_new_buf, value_new_buf, hidden_buf, keys_buf, values_buf, sems,
 ):
+    half = expert_down.shape[0] // lax.axis_size(axis)
+    first = pl.multiple_of(lax.axis_index(axis) * half, LANES)
     copies = [
         pltpu.make_async_copy(source, target, sems.at[slot])
         for slot, (source, target) in enumerate(
@@ -153,6 +156,7 @@
                 (values.at[0], values_buf),
                 (value_new, value_new_buf),
                 (hidden, hidden_buf),
+                (expert_down.at[pl.ds(first, down_head.shape[0])], down_head),
             )
         )
     ]
@@ -195,25 +199,30 @@
     copies[5].wait()
     own_value = per_head(value_new_buf[...].astype(jnp.float32), heads)
     attended = (per_head(mixed, heads) + own_weight * own_value).astype(jnp.bfloat16)
-    residual = per_head(hidden_buf[...].astype(jnp.float32), heads).astype(jnp.bfloat16)
-    message = jnp.concatenate([attended, residual], axis=0)
-    out[...] = jnp.broadcast_to(message[None], out.shape)
-
-
-def project_kernel(gathered, w_out, shared_up, shared_down, out, hidden_out):
+    pieces = per_head(hidden_buf[...].astype(jnp.float32), heads)
+    out[:, :heads, :] = jnp.broadcast_to(attended[None], (out.shape[0], heads, LANES))
+    extra = out.shape[1] - heads
+    for peer in range(out.shape[0]):
+        piece = jnp.broadcast_to(pieces[peer : peer + 1], (extra, LANES))
+        out[peer, heads:, :] = piece.astype(jnp.bfloat16)
+    copies[6].wait()
+
+
+def project_kernel(gathered, w_out, shared_up, shared_down, out):
     tokens, rows, _ = gathered.shape
-    total = tokens * rows
-    flat = gathered[...].reshape(total, LANES)
-    target = lax.broadcasted_iota(jnp.int32, (total, total), 0)
-    source = lax.broadcasted_iota(jnp.int32, (total, total), 1)
+    heads = w_out.shape[0] // LANES
+    flat = gathered[...].reshape(tokens * rows, LANES)
+    shape = (tokens * (heads + 1), tokens * rows)
+    target = lax.broadcasted_iota(jnp.int32, shape, 0)
+    source = lax.broadcasted_iota(jnp.int32, shape, 1)
     wanted = (target % tokens) * rows + target // tokens
     swap = jnp.where(source == wanted, 1.0, 0.0).astype(jnp.bfloat16)
-    swapped = jnp.dot(swap, flat, preferred_element_type=jnp.float32).astype(jnp.bfloat16)
-    blocks = [swapped[row * tokens : (row + 1) * tokens] for row in range(rows)]
-    attended = jnp.concatenate(blocks[: rows // 2], axis=1)
-    hidden_out[...] = jnp.concatenate(blocks[rows // 2 :], axis=1)
+    swapped = jnp.dot(swap, flat, preferred_element_type=jnp.float32)
+    blocks = [swapped[row * tokens : (row + 1) * tokens] for row in range(heads + 1)]
+    attended = jnp.concatenate(blocks[:heads], axis=1).astype(jnp.bfloat16)
     projected = jnp.dot(attended, w_out[...], preferred_element_type=jnp.float32)
-    out[...] = jnp.broadcast_to(projected.astype(jnp.bfloat16)[None], out.shape)
+    residual = blocks[heads] + projected.astype(jnp.bfloat16).astype(jnp.float32)
+    out[...] = jnp.broadcast_to(residual.astype(jnp.bfloat16)[None], out.shape)
 
 
 def gelu(value):
@@ -221,88 +230,121 @@
 
 
 def mlp_kernel(
-    axis, local_experts, up_step, down_step, slots,
-    routes, projected, hidden, ln_gain, router, shared_up, shared_down, expert_up, expert_down,
-    out, own_out,
-    router_buf, down_buf, act_buf, router_sem, down_sems,
-):
-    device_index = lax.axis_index(axis)
-    tokens, width = hidden.shape
-    columns = expert_up.shape[1]
-    units = columns // local_experts
-    down_count = columns // down_step
+    axes, up_step, down_step,
+    routes_in, residuals, ln_gain, router, shared_up, shared_down, expert_up, down_head,
+    expert_down, out, own_out,
+    routes, router_buf, down_buf, act_buf, terms_buf, sems, down_sems,
+):
+    group, member = (lax.axis_index(axis) for axis in axes)
+    groups, members = (lax.axis_size(axis) for axis in axes)
+    group_tokens = routes.shape[0]
+    tokens = groups * group_tokens
+    width = shared_up.shape[0]
+    blocks = width // LANES
+    columns = expert_up.shape[1] // groups
+    first_column = group * columns
+    head = down_head.shape[0]
+    down_count = (columns - head) // down_step
+
+    def part(start, size):
+        return pl.ds(pl.multiple_of(start, LANES), size)
 
     def down_copy(index):
-        slot = index % slots
         return pltpu.make_async_copy(
-            expert_down.at[index * down_step : (index + 1) * down_step],
-            down_buf.at[slot],
-            down_sems.at[slot],
-        )
-
-    router_copy = pltpu.make_async_copy(router, router_buf, router_sem)
+            expert_down.at[part(first_column + head + index * down_step, down_step)],
+            down_buf.at[index],
+            down_sems.at[index],
+        )
+
+    routes_copy = pltpu.make_async_copy(routes_in, routes, sems.at[0])
+    router_copy = pltpu.make_async_copy(router, router_buf, sems.at[1])
+    routes_copy.start()
     router_copy.start()
-    for index in range(min(slots, down_count)):
+
+    @pl.loop(0, down_count)
+    def _(index):
         down_copy(index).start()
 
-    blocks = width // LANES
-    every_projected = jnp.concatenate(
-        [projected[block].astype(jnp.float32) for block in range(projected.shape[0])], axis=1
-    )
-    residual = hidden[...].astype(jnp.float32) + every_projected
-    token = lax.broadcasted_iota(jnp.int32, (tokens, width), 0)
-    own = jnp.sum(jnp.where(token == device_index, residual, 0.0), axis=0, keepdims=True)
-    own_out[...] = per_head(own, blocks)
+    residual = jnp.concatenate(
+        [
+            jnp.concatenate(
+                [residuals[base + block].astype(jnp.float32) for block in range(blocks)], axis=1
+            )
+            for base in range(0, groups * members, members)
+        ],
+        axis=0,
+    )
     centered = residual - jnp.mean(residual, axis=1, keepdims=True)
     variance = jnp.mean(centered * centered, axis=1, keepdims=True)
     gain = ln_gain[...].astype(jnp.float32)
     gain = jnp.concatenate([gain[block : block + 1] for block in range(blocks)], axis=1)
     normed = (centered / jnp.sqrt(jnp.maximum(variance, 0.25)) * gain).astype(jnp.bfloat16)
+    for step in range(columns // up_step):
+        act_buf[:, step * up_step : (step + 1) * up_step] = gelu(
+            jnp.dot(
+                normed,
+                expert_up[:, part(first_column + step * up_step, up_step)],
+                preferred_element_type=jnp.float32,
+            )
+        )
+
+    here_normed = normed[:group_tokens]
+    for other in range(1, groups):
+        rows = normed[other * group_tokens : (other + 1) * group_tokens]
+        here_normed = jnp.where(group == other, rows, here_normed)
+    shared_act = gelu(jnp.dot(here_normed, shared_up[...], preferred_element_type=jnp.float32))
+    shared = jnp.dot(shared_act, shared_down[...], preferred_element_type=jnp.float32)
+    token = lax.broadcasted_iota(jnp.int32, (tokens, width), 0)
+    own = jnp.where(token == group * group_tokens + member, residual, 0.0)
+    own_out[:blocks] = per_head(jnp.sum(own, axis=0, keepdims=True), blocks)
 
     router_copy.wait()
+    routes_copy.wait()
     logits = lax.dot_general(
-        normed, router_buf[...], (((1,), (1,)), ((), ())), preferred_element_type=jnp.float32
-    )
-    experts = logits.shape[1]
-    token_column = lax.broadcasted_iota(jnp.int32, (tokens, 1), 0)
-    route = jnp.zeros((tokens, 1), jnp.int32)
-    for index in range(tokens):
+        here_normed, router_buf[...], (((1,), (1,)), ((), ())), preferred_element_type=jnp.float32
+    )
+    token_column = lax.broadcasted_iota(jnp.int32, (group_tokens, 1), 0)
+    route = jnp.zeros((group_tokens, 1), jnp.int32)
+    for index in range(group_tokens):
         route = jnp.where(token_column == index, routes[index], route)
-    expert_lane = lax.broadcasted_iota(jnp.int32, (tokens, experts), 1)
+    expert_lane = lax.broadcasted_iota(jnp.int32, logits.shape, 1)
     chosen = jnp.sum(jnp.where(expert_lane == route, logits, 0.0), axis=1, keepdims=True)
     gate = jax.nn.sigmoid(chosen)
-    shared_act = gelu(jnp.dot(normed, shared_up[...], preferred_element_type=jnp.float32))
-    total = jnp.dot(shared_act, shared_down[...], preferred_element_type=jnp.float32)
-
-    for expert in range(local_experts):
-        first = expert * (units // down_step)
-
-        for step in range(expert * units // up_step, (expert + 1) * units // up_step):
-            at = slice(step * up_step, (step + 1) * up_step)
-            act_buf[:, at] = gelu(
-                jnp.dot(normed, expert_up[:, at], preferred_element_type=jnp.float32)
-            )
-        sums = jnp.zeros((tokens, width), jnp.float32)
-        for index in range(first, first + units // down_step):
-            down_copy(index).wait()
-            at = slice(index * down_step, (index + 1) * down_step)
-            sums = sums + jnp.dot(
-                act_buf[:, at], down_buf[index % slots], preferred_element_type=jnp.float32
-            )
-            if index + slots < down_count:
-                down_copy(index + slots).start()
-        here = route == device_index * local_experts + expert
-        total = total + jnp.where(here, gate, 0.0) * sums
-
+    own_gate = jnp.sum(jnp.where(token_column == member, gate, 0.0), axis=0, keepdims=True)
+    own_route = jnp.sum(jnp.where(token_column == member, route, 0), axis=0, keepdims=True)
+    holder = lax.rem(own_route, groups)
+    own_holder = holder * members + own_route // groups
+    away = jnp.where(holder == group, 0.0, own_gate)
+    source = lax.broadcasted_iota(jnp.int32, (groups * members, LANES), 0)
+    own_out[blocks:] = jnp.where(
+        source // members == group, 1.0, jnp.where(source == own_holder, away, 0.0)
+    )
+
+    sums = jnp.dot(act_buf[:, :head], down_head[...], preferred_element_type=jnp.float32)
+    for index in range(down_count):
+        down_copy(index).wait()
+        at = slice(head + index * down_step, head + (index + 1) * down_step)
+        sums = sums + jnp.dot(
+            act_buf[:, at], down_buf[index], preferred_element_type=jnp.float32
+        )
+    here_gate = jnp.where(route == member * groups + group, gate, 0.0)
+    parts = []
+    for other in range(groups):
+        rows = sums[other * group_tokens : (other + 1) * group_tokens]
+        parts.append(jnp.where(group == other, shared + here_gate * rows, rows))
+    total = jnp.concatenate(parts, axis=0)
     for block in range(blocks):
-        out[:, block, :] = total[:, block * LANES : (block + 1) * LANES]
+        terms_buf[:, block, :] = total[:, block * LANES : (block + 1) * LANES]
+    out[...] = terms_buf[...].astype(out.dtype)
 
 
 def combine_kernel(terms, own, out):
-    total = own[...]
+    blocks = terms.shape[1]
+    total = own[:blocks]
     for index in range(terms.shape[0]):
-        total = total + terms[index]
-    for block in range(total.shape[0]):
+        scale = own[blocks + index : blocks + index + 1]
+        total = total + scale * terms[index].astype(jnp.float32)
+    for block in range(blocks):
         out[:, block * LANES : (block + 1) * LANES] = total[block : block + 1].astype(out.dtype)
 
 
@@ -320,33 +362,37 @@
 
 
 def mlp(
-    routes, projected, hidden, ln_gain, router, shared_up, shared_down, expert_up, expert_down
-):
-    tokens, width = hidden.shape
+    routes, residuals, ln_gain, router, shared_up, shared_down, expert_up, down_head, expert_down
+):
+    tokens = residuals.shape[0]
+    width, columns = expert_up.shape
     blocks = width // LANES
-    columns = expert_up.shape[1]
-    local_experts = columns // FF
-    slots, down_step, up_step = 9, 512, 1024
+    columns = columns // lax.axis_size("group")
+    down_step, up_step = 512, 1024
+    down_count = (columns - down_head.shape[0]) // down_step
     return pl.pallas_call(
-        functools.partial(mlp_kernel, "expert", local_experts, up_step, down_step, slots),
+        functools.partial(mlp_kernel, ("group", "expert"), up_step, down_step),
         out_shape=(
-            pltpu.VMEM((tokens, blocks, LANES), jnp.float32),
-            pltpu.VMEM((blocks, LANES), jnp.float32),
+            pltpu.VMEM((tokens, blocks, LANES), jnp.bfloat16),
+            pltpu.VMEM((blocks + tokens, LANES), jnp.float32),
         ),
-        in_specs=[SMEM, VMEM, VMEM, VMEM, HBM, VMEM, VMEM, VMEM, HBM],
+        in_specs=[HBM, VMEM, VMEM, HBM, VMEM, VMEM, VMEM, VMEM, HBM],
         out_specs=(VMEM, VMEM),
         scratch_shapes=[
+            pltpu.SMEM(routes.shape, routes.dtype),
             pltpu.VMEM(router.shape, router.dtype),
-            pltpu.VMEM((slots, down_step, width), expert_down.dtype),
+            pltpu.VMEM((down_count, down_step, width), expert_down.dtype),
             pltpu.VMEM((tokens, columns), jnp.bfloat16),
-            pltpu.SemaphoreType.DMA,
-            pltpu.SemaphoreType.DMA((slots,)),
+            pltpu.VMEM((tokens, blocks, LANES), jnp.float32),
+            pltpu.SemaphoreType.DMA((2,)),
+            pltpu.SemaphoreType.DMA((down_count,)),
         ],
-        compiler_params=params(25),
+        compiler_params=params(17),
         cost_estimate=cost(10**11),
         name="mlp",
     )(
-        routes, projected, hidden, ln_gain, router, shared_up, shared_down, expert_up, expert_down
+        routes, residuals, ln_gain, router, shared_up, shared_down, expert_up, down_head,
+        expert_down,
     )
 
 
@@ -358,48 +404,50 @@
     blocks = width // LANES
     cache_len = key_cache.shape[1]
     tokens = routes.shape[0]
+    both = ("group", "expert")
+    groups = lax.axis_size("group")
     in_hbm = functools.partial(pltpu.with_memory_space_constraint, memory_space=pltpu.HBM)
+    in_vmem = functools.partial(pltpu.with_memory_space_constraint, memory_space=pltpu.VMEM)
     query, key_new, value_new, key_cache, value_cache, hidden = map(
         in_hbm, (query, key_new, value_new, key_cache, value_cache, hidden)
     )
-    in_vmem = functools.partial(pltpu.with_memory_space_constraint, memory_space=pltpu.VMEM)
     router, expert_down = map(in_hbm, (router.T, expert_down))
     shared_up, shared_down, expert_up = map(in_vmem, (shared_up, shared_down, expert_up))
     row = pltpu.VMEM((1, width), jnp.bfloat16)
     cache = pltpu.VMEM((cache_len, width), jnp.bfloat16)
-    message = pl.pallas_call(
-        attend_kernel,
-        out_shape=jax.ShapeDtypeStruct((tokens, 2 * blocks, LANES), jnp.bfloat16),
-        in_specs=[SMEM] + [HBM] * 6,
-        out_specs=VMEM,
-        scratch_shapes=[row] * 4 + [cache] * 2 + [pltpu.SemaphoreType.DMA((6,))],
+    message, down_head = pl.pallas_call(
+        functools.partial(attend_kernel, "group"),
+        out_shape=(
+            pltpu.VMEM((tokens, blocks + 8, LANES), jnp.bfloat16),
+            pltpu.VMEM((HEAD_ROWS, width), expert_down.dtype),
+        ),
+        in_specs=[SMEM] + [HBM] * 7,
+        out_specs=(VMEM, VMEM),
+        scratch_shapes=[row] * 4 + [cache] * 2 + [pltpu.SemaphoreType.DMA((7,))],
         compiler_params=params(4),
         cost_estimate=cost(10**11),
         name="attend",
-    )(lengths, query, key_new, value_new, key_cache, value_cache, hidden)
+    )(lengths, query, key_new, value_new, key_cache, value_cache, hidden, expert_down)
     gathered = lax.all_to_all(message, "expert", 0, 0)
-    message, every_hidden = pl.pallas_call(
+    message = pl.pallas_call(
         project_kernel,
-        out_shape=(
-            jax.ShapeDtypeStruct((tokens, tokens, LANES), jnp.bfloat16),
-            jax.ShapeDtypeStruct((tokens, width), jnp.bfloat16),
-        ),
+        out_shape=jax.ShapeDtypeStruct((groups * tokens, tokens, LANES), jnp.bfloat16),
         in_specs=[VMEM] * 4,
-        out_specs=(VMEM, VMEM),
+        out_specs=VMEM,
         compiler_params=params(4),
         cost_estimate=cost(10**11),
         name="project",
     )(gathered, w_out, shared_up, shared_down)
-    every_projected = lax.all_to_all(message, "expert", 0, 0)
+    residuals = lax.all_to_all(message, both, 0, 0)
     terms, own = mlp(
-        routes, in_vmem(every_projected), in_vmem(every_hidden), ln_gain.reshape(blocks, LANES), router,
-        shared_up, shared_down, expert_up, expert_down,
-    )
-    terms = lax.all_to_all(terms, "expert", 0, 0)
+        in_hbm(routes), in_vmem(residuals), in_vmem(ln_gain.reshape(blocks, LANES)), router,
+        shared_up, shared_down, expert_up, in_vmem(down_head), expert_down,
+    )
+    terms = lax.all_to_all(terms, both, 0, 0)
     return pl.pallas_call(
         combine_kernel,
         out_shape=jax.ShapeDtypeStruct((1, width), jnp.bfloat16),
-        in_specs=[VMEM] * 2,
+        in_specs=[VMEM, VMEM],
         out_specs=VMEM,
         compiler_params=params(2),
         name="combine",
@@ -415,7 +463,8 @@
         and HEAD_DIM == LANES
         and w_out.shape[1] == LANES
         and tokens * LANES == query.shape[1]
-        and rest[4].shape[1] % FF == 0
+        and lax.axis_size("group") == 2
+        and rest[4].shape[1] == 2 * FF
     )
 
 

time: 52.5 us -> 47.6 us (0.907)
  Pallas kernels: 15.7 us -> 11.7 us
  blocking collectives: 35.6 us -> 34.9 us
    pallas_call x3, Pallas kernels: 15.1 us -> 11.1 us  [the longest x1 7.51 us: mlp(): pl.pallas_call(functools.partial(mlp_kernel, ('group', 'expert'), up_step...]
where the time goes in v3:
time: 47.6 us; the launch traced here: 47.4 us
  blocking collectives  34.9 us (73%)
  Pallas kernels  11.7 us (25%)
  between operations  0.72 us (2%)
    all_to_all x1, blocking collectives, fast_body(): gathered = lax.all_to_all(message, 'expert', 0, 0)  14.7 us
    all_to_all x1, blocking collectives, fast_body(): residuals = lax.all_to_all(message, both, 0, 0)  10.2 us
    all_to_all x1, blocking collectives, fast_body(): terms = lax.all_to_all(terms, both, 0, 0)  9.98 us
    pallas_call x1, Pallas kernels, mlp(): pl.pallas_call(functools.partial(mlp_kernel, ('group', 'expert'), up_step...  7.51 us
    pallas_call x1, Pallas kernels, fast_body(): pl.pallas_call(functools.partial(attend_kernel, 'group'), out_shape=(pltp...  3.08 us

profile of v3, /device:TPU:0, one launch (start us, length us, event | category | flops | bytes accessed | tf_op | source)
XLA Modules:
  0.0 47.4 jit_solution(9439092776320346599)
XLA Ops:
  0.7 0.0 copy-start.1
  0.7 0.0 copy-start.2
  0.7 0.0 copy-start.3
  0.7 3.1 %attend.1 = (bf16[16,24,128]{2,1,0:T(8,128)(2,1)S(1)}, bf16[1024,2048]{1,0:T(8,128)(2,1)S(1)}) custom-call(s32[1]{0:T(128)S(6)} %copy.16.lengths, bf16[1,2048]{1,0:T(2,128)(2,1)} %query.1, bf16[1,2048]{1,0:T(2,128)(2,1)} %key_new.1, bf16[1,2048]{1,0:T(2,128)(2,1)} %value_new.1, bf16[1,256,2048]{2,1,0:T(8,128)(2,1)} %keys.1, bf16[1,256,2048]{2,1,0:T(8,128)(2,1)} %values.1, ...), custom_call_target="tpu_custom_call" | custom-call | flops 99999997952 | bytes 390624992 | tf_op jit(solution)/shard_map/attend/pallas_call | solution.py:418
  3.8 14.7 %all_to_all.15.gathered = bf16[16,24,128]{2,1,0:T(8,128)(2,1)S(1)} all-to-all(bf16[16,24,128]{2,1,0:T(8,128)(2,1)S(1)} %get-tuple-element.9), channel_id=1, replica_groups=mesh['group'=2,'expert'=16] {'expert'}, dimensions={0} | all-to-all | bytes 196608 | tf_op jit(solution)/shard_map/all_to_all | solution.py:431
  18.5 0.0 copy-done.1
  18.5 0.0 copy-done.2
  18.5 0.0 copy-done.3
  18.5 0.0 copy-start
  18.5 0.0 copy-start.4
  18.5 0.5 %project.1 = bf16[32,16,128]{2,1,0:T(8,128)(2,1)S(1)} custom-call(bf16[16,24,128]{2,1,0:T(8,128)(2,1)S(1)} %all_to_all.15.gathered, bf16[2048,128]{1,0:T(8,128)(2,1)S(1)} %copy-done.3, bf16[2048,512]{1,0:T(8,128)(2,1)S(1)} %copy-done.1, bf16[512,2048]{1,0:T(8,128)(2,1)S(1)} %copy-done.2), custom_call_target="tpu_custom_call" | custom-call | flops 99999997952 | bytes 390624992 | tf_op jit(solution)/shard_map/project/pallas_call | solution.py:432
  19.0 10.2 %all_to_all.16.residuals = bf16[32,16,128]{2,1,0:T(8,128)(2,1)S(1)} all-to-all(bf16[32,16,128]{2,1,0:T(8,128)(2,1)S(1)} %project.1), channel_id=1, replica_groups=mesh['group'=2,'expert'=16] {'group','expert'}, dimensions={0} | all-to-all | bytes 262144 | tf_op jit(solution)/shard_map/all_to_all | solution.py:441
  29.2 0.0 copy-done
  29.2 0.0 copy-done.4
  29.2 7.5 %mlp.1 = (bf16[32,16,128]{2,1,0:T(8,128)(2,1)S(1)}, f32[48,128]{1,0:T(8,128)S(1)}) custom-call(s32[16]{0:T(128)} %routes_in.1, bf16[32,16,128]{2,1,0:T(8,128)(2,1)S(1)} %all_to_all.16.residuals, bf16[16,128]{1,0:T(8,128)(2,1)S(1)} %bitcast.2, bf16[32,2048]{1,0:T(8,128)(2,1)} %bitcast.3, bf16[2048,512]{1,0:T(8,128)(2,1)S(1)} %copy-done.1, ...), custom_call_target="tpu_custom_call" | custom-call | flops 99999997952 | bytes 390624992 | tf_op jit(solution)/shard_map/mlp/pallas_call | solution.py:373
  36.7 10.0 %all_to_all.17.terms = bf16[32,16,128]{2,1,0:T(8,128)(2,1)S(1)} all-to-all(bf16[32,16,128]{2,1,0:T(8,128)(2,1)S(1)} %get-tuple-element.11), channel_id=1, replica_groups=mesh['group'=2,'expert'=16] {'group','expert'}, dimensions={0} | all-to-all | bytes 262144 | tf_op jit(solution)/shard_map/all_to_all | solution.py:446
  46.7 0.7 %combine.1 = bf16[1,2048]{1,0:T(2,128)(2,1)} custom-call(bf16[32,16,128]{2,1,0:T(8,128)(2,1)S(1)} %all_to_all.17.terms, f32[48,128]{1,0:T(8,128)S(1)} %get-tuple-element.12.own), custom_call_target="tpu_custom_call" | custom-call | tf_op jit(solution)/shard_map/combine/pallas_call | solution.py:447
Async XLA Ops:
  0.7 17.8 %copy-start.1 = (bf16[2048,512]{1,0:T(8,128)(2,1)S(1)}, bf16[2048,512]{1,0:T(8,128)(2,1)}, u32[]{:S(2)}) copy-start(bf16[2048,512]{1,0:T(8,128)(2,1)} %shared_up.3) | copy-start | bytes 6291460
  0.7 17.8 %copy-start.2 = (bf16[512,2048]{1,0:T(8,128)(2,1)S(1)}, bf16[512,2048]{1,0:T(8,128)(2,1)}, u32[]{:S(2)}) copy-start(bf16[512,2048]{1,0:T(8,128)(2,1)} %shared_down.3) | copy-start | bytes 6291460
  0.7 17.8 %copy-start.3 = (bf16[2048,128]{1,0:T(8,128)(2,1)S(1)}, bf16[2048,128]{1,0:T(8,128)(2,1)}, u32[]{:S(2)}) copy-start(bf16[2048,128]{1,0:T(8,128)(2,1)} %w_out.1) | copy-start | bytes 1572868
  18.5 10.7 %copy-start = (bf16[2048,8192]{1,0:T(8,128)(2,1)S(1)}, bf16[2048,8192]{1,0:T(8,128)(2,1)}, u32[]{:S(2)}) copy-start(bf16[2048,8192]{1,0:T(8,128)(2,1)} %expert_up.1) | copy-start | bytes 100663296
  18.5 10.7 %copy-start.4 = (bf16[2048]{0:T(1024)(128)(2,1)S(1)}, bf16[2048]{0:T(1024)(128)(2,1)}, u32[]{:S(2)}) copy-start(bf16[2048]{0:T(1024)(128)(2,1)} %param.24) | copy-start | bytes 12292

commit v4 on v3

--- a/solution.py
+++ b/solution.py
@@ -128,7 +128,8 @@
 
 
 LANES = 128
-HEAD_ROWS = 1024
+HEAD_ROWS = 512
+PIECES = (1536, 1024, 512, 512)
 
 
 def per_head(row, heads):
@@ -229,11 +230,15 @@
     return jax.nn.gelu(value, approximate=True).astype(jnp.bfloat16)
 
 
+def part_of(group, members):
+    return pl.ds(group * members, members)
+
+
 def mlp_kernel(
-    axes, up_step, down_step,
+    axes, up_step, pieces,
     routes_in, residuals, ln_gain, router, shared_up, shared_down, expert_up, down_head,
     expert_down, out, own_out,
-    routes, router_buf, down_buf, act_buf, terms_buf, sems, down_sems,
+    routes, down_buf, act_buf, terms_buf, routes_sem, down_sems,
 ):
     group, member = (lax.axis_index(axis) for axis in axes)
     groups, members = (lax.axis_size(axis) for axis in axes)
@@ -244,24 +249,23 @@
     columns = expert_up.shape[1] // groups
     first_column = group * columns
     head = down_head.shape[0]
-    down_count = (columns - head) // down_step
+    step_rows = pieces[-1]
 
     def part(start, size):
         return pl.ds(pl.multiple_of(start, LANES), size)
 
     def down_copy(index):
+        rows = part(index * step_rows, step_rows)
         return pltpu.make_async_copy(
-            expert_down.at[part(first_column + head + index * down_step, down_step)],
-            down_buf.at[index],
+            expert_down.at[part(first_column + head + index * step_rows, step_rows)],
+            down_buf.at[rows],
             down_sems.at[index],
         )
 
-    routes_copy = pltpu.make_async_copy(routes_in, routes, sems.at[0])
-    router_copy = pltpu.make_async_copy(router, router_buf, sems.at[1])
+    routes_copy = pltpu.make_async_copy(routes_in, routes, routes_sem)
     routes_copy.start()
-    router_copy.start()
-
-    @pl.loop(0, down_count)
+
+    @pl.loop(0, (columns - head) // step_rows)
     def _(index):
         down_copy(index).start()
 
@@ -274,11 +278,14 @@
         ],
         axis=0,
     )
-    centered = residual - jnp.mean(residual, axis=1, keepdims=True)
+    mean = jnp.mean(residual, axis=1, keepdims=True)
+    centered = residual - mean
     variance = jnp.mean(centered * centered, axis=1, keepdims=True)
     gain = ln_gain[...].astype(jnp.float32)
     gain = jnp.concatenate([gain[block : block + 1] for block in range(blocks)], axis=1)
-    normed = (centered / jnp.sqrt(jnp.maximum(variance, 0.25)) * gain).astype(jnp.bfloat16)
+    normed = (centered * (1.0 / jnp.sqrt(jnp.maximum(variance, 0.25))) * gain).astype(
+        jnp.bfloat16
+    )
     for step in range(columns // up_step):
         act_buf[:, step * up_step : (step + 1) * up_step] = gelu(
             jnp.dot(
@@ -294,15 +301,15 @@
         here_normed = jnp.where(group == other, rows, here_normed)
     shared_act = gelu(jnp.dot(here_normed, shared_up[...], preferred_element_type=jnp.float32))
     shared = jnp.dot(shared_act, shared_down[...], preferred_element_type=jnp.float32)
-    token = lax.broadcasted_iota(jnp.int32, (tokens, width), 0)
-    own = jnp.where(token == group * group_tokens + member, residual, 0.0)
-    own_out[:blocks] = per_head(jnp.sum(own, axis=0, keepdims=True), blocks)
-
-    router_copy.wait()
+    logits = lax.dot_general(
+        here_normed, router[...], (((1,), (1,)), ((), ())), preferred_element_type=jnp.float32
+    )
+    here = residuals[part_of(group, members)].astype(jnp.float32)
+    token = lax.broadcasted_iota(jnp.int32, here.shape, 1)
+    own_out[:blocks] = jnp.sum(jnp.where(token == member, here, 0.0), axis=1)
+    sums = jnp.dot(act_buf[:, :head], down_head[...], preferred_element_type=jnp.float32)
+
     routes_copy.wait()
-    logits = lax.dot_general(
-        here_normed, router_buf[...], (((1,), (1,)), ((), ())), preferred_element_type=jnp.float32
-    )
     token_column = lax.broadcasted_iota(jnp.int32, (group_tokens, 1), 0)
     route = jnp.zeros((group_tokens, 1), jnp.int32)
     for index in range(group_tokens):
@@ -320,13 +327,16 @@
         source // members == group, 1.0, jnp.where(source == own_holder, away, 0.0)
     )
 
-    sums = jnp.dot(act_buf[:, :head], down_head[...], preferred_element_type=jnp.float32)
-    for index in range(down_count):
-        down_copy(index).wait()
-        at = slice(head + index * down_step, head + (index + 1) * down_step)
+    first = 0
+    for size in pieces:
+        for index in range(first // step_rows, (first + size) // step_rows):
+            down_copy(index).wait()
         sums = sums + jnp.dot(
-            act_buf[:, at], down_buf[index], preferred_element_type=jnp.float32
+            act_buf[:, head + first : head + first + size],
+            down_buf[first : first + size],
+            preferred_element_type=jnp.float32,
         )
+        first += size
     here_gate = jnp.where(route == member * groups + group, gate, 0.0)
     parts = []
     for other in range(groups):
@@ -368,26 +378,25 @@
     width, columns = expert_up.shape
     blocks = width // LANES
     columns = columns // lax.axis_size("group")
-    down_step, up_step = 512, 1024
-    down_count = (columns - down_head.shape[0]) // down_step
+    up_step, pieces = 1024, PIECES
+    rows = columns - down_head.shape[0]
     return pl.pallas_call(
-        functools.partial(mlp_kernel, ("group", "expert"), up_step, down_step),
+        functools.partial(mlp_kernel, ("group", "expert"), up_step, pieces),
         out_shape=(
             pltpu.VMEM((tokens, blocks, LANES), jnp.bfloat16),
             pltpu.VMEM((blocks + tokens, LANES), jnp.float32),
         ),
-        in_specs=[HBM, VMEM, VMEM, HBM, VMEM, VMEM, VMEM, VMEM, HBM],
+        in_specs=[HBM, VMEM, VMEM, VMEM, VMEM, VMEM, VMEM, VMEM, HBM],
         out_specs=(VMEM, VMEM),
         scratch_shapes=[
             pltpu.SMEM(routes.shape, routes.dtype),
-            pltpu.VMEM(router.shape, router.dtype),
-            pltpu.VMEM((down_count, down_step, width), expert_down.dtype),
+            pltpu.VMEM((rows, width), expert_down.dtype),
             pltpu.VMEM((tokens, columns), jnp.bfloat16),
             pltpu.VMEM((tokens, blocks, LANES), jnp.float32),
-            pltpu.SemaphoreType.DMA((2,)),
-            pltpu.SemaphoreType.DMA((down_count,)),
+            pltpu.SemaphoreType.DMA,
+            pltpu.SemaphoreType.DMA((rows // pieces[-1],)),
         ],
-        compiler_params=params(17),
+        compiler_params=params(19),
         cost_estimate=cost(10**11),
         name="mlp",
     )(
@@ -411,8 +420,10 @@
     query, key_new, value_new, key_cache, value_cache, hidden = map(
         in_hbm, (query, key_new, value_new, key_cache, value_cache, hidden)
     )
-    router, expert_down = map(in_hbm, (router.T, expert_down))
-    shared_up, shared_down, expert_up = map(in_vmem, (shared_up, shared_down, expert_up))
+    expert_down = in_hbm(expert_down)
+    shared_up, shared_down, expert_up, router = map(
+        in_vmem, (shared_up, shared_down, expert_up, router.T)
+    )
     row = pltpu.VMEM((1, width), jnp.bfloat16)
     cache = pltpu.VMEM((cache_len, width), jnp.bfloat16)
     message, down_head = pl.pallas_call(

time: 47.6 us -> 46.8 us (0.983)
  Pallas kernels: 11.7 us -> 11 us
    pallas_call x1, Pallas kernels: 3.08 us -> 2.57 us  [fast_body(): pl.pallas_call(functools.partial(attend_kernel, 'group'), out_shape=(pltp...]
where the time goes in v4:
time: 46.8 us; the launch traced here: 46.6 us
  blocking collectives  34.8 us (74%)
  Pallas kernels  11 us (24%)
  between operations  0.73 us (2%)
    all_to_all x1, blocking collectives, fast_body(): gathered = lax.all_to_all(message, 'expert', 0, 0)  14.7 us
    all_to_all x1, blocking collectives, fast_body(): residuals = lax.all_to_all(message, both, 0, 0)  10.2 us
    all_to_all x1, blocking collectives, fast_body(): terms = lax.all_to_all(terms, both, 0, 0)  9.95 us
    pallas_call x1, Pallas kernels, mlp(): pl.pallas_call(functools.partial(mlp_kernel, ('group', 'expert'), up_step...  7.31 us
    pallas_call x1, Pallas kernels, fast_body(): pl.pallas_call(functools.partial(attend_kernel, 'group'), out_shape=(pltp...  2.57 us

profile of v4, /device:TPU:0, one launch (start us, length us, event | category | flops | bytes accessed | tf_op | source)
XLA Modules:
  0.0 46.6 jit_solution(10816412809930444508)
XLA Ops:
  0.7 0.0 copy-start.1
  0.7 0.0 copy-start.2
  0.7 0.0 copy-start.3
  0.7 2.6 %attend.1 = (bf16[16,24,128]{2,1,0:T(8,128)(2,1)S(1)}, bf16[512,2048]{1,0:T(8,128)(2,1)S(1)}) custom-call(s32[1]{0:T(128)S(6)} %copy.16.lengths, bf16[1,2048]{1,0:T(2,128)(2,1)} %query.1, bf16[1,2048]{1,0:T(2,128)(2,1)} %key_new.1, bf16[1,2048]{1,0:T(2,128)(2,1)} %value_new.1, bf16[1,256,2048]{2,1,0:T(8,128)(2,1)} %keys.1, bf16[1,256,2048]{2,1,0:T(8,128)(2,1)} %values.1, ...), custom_call_target="tpu_custom_call" | custom-call | flops 99999997952 | bytes 390624992 | tf_op jit(solution)/shard_map/attend/pallas_call | solution.py:429
  3.3 14.7 %all_to_all.15.gathered = bf16[16,24,128]{2,1,0:T(8,128)(2,1)S(1)} all-to-all(bf16[16,24,128]{2,1,0:T(8,128)(2,1)S(1)} %get-tuple-element.9), channel_id=1, replica_groups=mesh['group'=2,'expert'=16] {'expert'}, dimensions={0} | all-to-all | bytes 196608 | tf_op jit(solution)/shard_map/all_to_all | solution.py:442
  18.0 0.0 copy-done.1
  18.0 0.0 copy-done.2
  18.0 0.0 copy-done.3
  18.0 0.0 copy-start
  18.0 0.0 copy-start.4
  18.0 0.0 copy-start.5
  18.0 0.5 %project.1 = bf16[32,16,128]{2,1,0:T(8,128)(2,1)S(1)} custom-call(bf16[16,24,128]{2,1,0:T(8,128)(2,1)S(1)} %all_to_all.15.gathered, bf16[2048,128]{1,0:T(8,128)(2,1)S(1)} %copy-done.3, bf16[2048,512]{1,0:T(8,128)(2,1)S(1)} %copy-done.1, bf16[512,2048]{1,0:T(8,128)(2,1)S(1)} %copy-done.2), custom_call_target="tpu_custom_call" | custom-call | flops 99999997952 | bytes 390624992 | tf_op jit(solution)/shard_map/project/pallas_call | solution.py:443
  18.5 10.2 %all_to_all.16.residuals = bf16[32,16,128]{2,1,0:T(8,128)(2,1)S(1)} all-to-all(bf16[32,16,128]{2,1,0:T(8,128)(2,1)S(1)} %project.1), channel_id=1, replica_groups=mesh['group'=2,'expert'=16] {'group','expert'}, dimensions={0} | all-to-all | bytes 262144 | tf_op jit(solution)/shard_map/all_to_all | solution.py:452
  28.7 0.0 copy-done
  28.7 0.0 copy-done.4
  28.7 0.0 copy-done.5
  28.7 7.3 %mlp.1 = (bf16[32,16,128]{2,1,0:T(8,128)(2,1)S(1)}, f32[48,128]{1,0:T(8,128)S(1)}) custom-call(s32[16]{0:T(128)} %routes_in.1, bf16[32,16,128]{2,1,0:T(8,128)(2,1)S(1)} %all_to_all.16.residuals, bf16[16,128]{1,0:T(8,128)(2,1)S(1)} %bitcast.3, bf16[32,2048]{1,0:T(8,128)(2,1)S(1)} %bitcast.2, bf16[2048,512]{1,0:T(8,128)(2,1)S(1)} %copy-done.1, ...), custom_call_target="tpu_custom_call" | custom-call | flops 99999997952 | bytes 390624992 | tf_op jit(solution)/shard_map/mlp/pallas_call | solution.py:383
  36.0 9.9 %all_to_all.17.terms = bf16[32,16,128]{2,1,0:T(8,128)(2,1)S(1)} all-to-all(bf16[32,16,128]{2,1,0:T(8,128)(2,1)S(1)} %get-tuple-element.11), channel_id=1, replica_groups=mesh['group'=2,'expert'=16] {'group','expert'}, dimensions={0} | all-to-all | bytes 262144 | tf_op jit(solution)/shard_map/all_to_all | solution.py:457
  46.0 0.7 %combine.1 = bf16[1,2048]{1,0:T(2,128)(2,1)} custom-call(bf16[32,16,128]{2,1,0:T(8,128)(2,1)S(1)} %all_to_all.17.terms, f32[48,128]{1,0:T(8,128)S(1)} %get-tuple-element.12.own), custom_call_target="tpu_custom_call" | custom-call | tf_op jit(solution)/shard_map/combine/pallas_call | solution.py:458
Async XLA Ops:
  0.7 17.3 %copy-start.1 = (bf16[2048,512]{1,0:T(8,128)(2,1)S(1)}, bf16[2048,512]{1,0:T(8,128)(2,1)}, u32[]{:S(2)}) copy-start(bf16[2048,512]{1,0:T(8,128)(2,1)} %shared_up.3) | copy-start | bytes 6291460
  0.7 17.3 %copy-start.2 = (bf16[512,2048]{1,0:T(8,128)(2,1)S(1)}, bf16[512,2048]{1,0:T(8,128)(2,1)}, u32[]{:S(2)}) copy-start(bf16[512,2048]{1,0:T(8,128)(2,1)} %shared_down.3) | copy-start | bytes 6291460
  0.7 17.3 %copy-start.3 = (bf16[2048,128]{1,0:T(8,128)(2,1)S(1)}, bf16[2048,128]{1,0:T(8,128)(2,1)}, u32[]{:S(2)}) copy-start(bf16[2048,128]{1,0:T(8,128)(2,1)} %w_out.1) | copy-start | bytes 1572868
  18.0 10.7 %copy-start = (bf16[2048,8192]{1,0:T(8,128)(2,1)S(1)}, bf16[2048,8192]{1,0:T(8,128)(2,1)}, u32[]{:S(2)}) copy-start(bf16[2048,8192]{1,0:T(8,128)(2,1)} %expert_up.1) | copy-start | bytes 100663296
  18.0 10.7 %copy-start.4 = (bf16[2048,32]{0,1:T(8,128)(2,1)S(1)}, bf16[2048,32]{0,1:T(8,128)(2,1)}, u32[]{:S(2)}) copy-start(bf16[2048,32]{0,1:T(8,128)(2,1)} %param.25) | copy-start | bytes 393220
  18.0 10.7 %copy-start.5 = (bf16[2048]{0:T(1024)(128)(2,1)S(1)}, bf16[2048]{0:T(1024)(128)(2,1)}, u32[]{:S(2)}) copy-start(bf16[2048]{0:T(1024)(128)(2,1)} %param.24) | copy-start | bytes 12292

commit v5 on v4

--- a/solution.py
+++ b/solution.py
@@ -209,6 +209,10 @@
     copies[6].wait()
 
 
+def hand_on_kernel(source, out):
+    out[0, 0:8] = source[0, 0:8]
+
+
 def project_kernel(gathered, w_out, shared_up, shared_down, out):
     tokens, rows, _ = gathered.shape
     heads = w_out.shape[0] // LANES
@@ -230,12 +234,47 @@
     return jax.nn.gelu(value, approximate=True).astype(jnp.bfloat16)
 
 
+TILE = 256
+
+
+def stream(jobs):
+    lanes = [[job for job in jobs if job[0] == unit] for unit in range(2)]
+    longest = max(len(lane) for lane in lanes)
+    for step in range(longest + 1):
+        for unit, lane in enumerate(lanes):
+            if step < len(lane):
+                pltpu.matmul_push_rhs(
+                    lane[step][3](), staging_register=step % 2, mxu_index=unit
+                )
+        for unit, lane in enumerate(lanes):
+            if 0 < step <= len(lane):
+                _, acc, rows, _, after = lane[step - 1]
+                pltpu.matmul_acc_lhs(acc, rows(), load_staged_rhs=(step - 1) % 2)
+                if after is not None:
+                    after()
+
+
 def part_of(group, members):
     return pl.ds(group * members, members)
 
 
-def mlp_kernel(
-    axes, up_step, pieces,
+def mlp_kernel(axes, pieces, *refs):
+    tokens, blocks = refs[9].shape[0], refs[9].shape[1]
+    wide = blocks * LANES // TILE // 2
+
+    def accumulators(rows, count):
+        return tuple((pltpu.ACC(q)((rows, TILE), jnp.float32),) * count for q in range(2))
+
+    pl.run_scoped(
+        lambda *accs: mlp_body(axes, pieces, accs, *refs),
+        accumulators(tokens, 2),
+        accumulators(tokens, wide),
+        accumulators(tokens // 2, wide),
+    )
+
+
+def mlp_body(
+    axes, pieces, accs,
     routes_in, residuals, ln_gain, router, shared_up, shared_down, expert_up, down_head,
     expert_down, out, own_out,
     routes, down_buf, act_buf, terms_buf, routes_sem, down_sems,
@@ -286,38 +325,111 @@
     normed = (centered * (1.0 / jnp.sqrt(jnp.maximum(variance, 0.25))) * gain).astype(
         jnp.bfloat16
     )
-    for step in range(columns // up_step):
-        act_buf[:, step * up_step : (step + 1) * up_step] = gelu(
-            jnp.dot(
-                normed,
-                expert_up[:, part(first_column + step * up_step, up_step)],
-                preferred_element_type=jnp.float32,
+    depth = width // TILE
+    up_accs, down_accs, small_accs = accs
+    for kind in accs:
+        for unit_accs in kind:
+            for acc in unit_accs:
+                pltpu.matmul_pop(acc)
+
+    def wide(start):
+        return part(start, TILE)
+
+    def up_jobs(column, spare):
+        unit = column % 2
+        acc = up_accs[unit][spare]
+
+        def finish():
+            act_buf[:, column * TILE : (column + 1) * TILE] = gelu(pltpu.matmul_pop(acc))
+
+        def job(k):
+            return (
+                unit,
+                acc,
+                lambda: normed[:, k * TILE : (k + 1) * TILE],
+                lambda: expert_up[
+                    k * TILE : (k + 1) * TILE, wide(first_column + column * TILE)
+                ],
+                finish if k == depth - 1 else None,
             )
-        )
+
+        return [job(k) for k in range(depth)]
+
+    stream([job for column in range(columns // TILE) for job in up_jobs(column, column // 2 % 2)])
 
     here_normed = normed[:group_tokens]
     for other in range(1, groups):
         rows = normed[other * group_tokens : (other + 1) * group_tokens]
         here_normed = jnp.where(group == other, rows, here_normed)
-    shared_act = gelu(jnp.dot(here_normed, shared_up[...], preferred_element_type=jnp.float32))
-    shared = jnp.dot(shared_act, shared_down[...], preferred_element_type=jnp.float32)
-    logits = lax.dot_general(
-        here_normed, router[...], (((1,), (1,)), ((), ())), preferred_element_type=jnp.float32
-    )
+    shared_units = shared_up.shape[1]
+    shared_act = []
+
+    def shared_up_job(column, k):
+        acc = small_accs[column % 2][column // 2]
+        return (
+            column % 2,
+            acc,
+            lambda: here_normed[:, k * TILE : (k + 1) * TILE],
+            lambda: shared_up[k * TILE : (k + 1) * TILE, column * TILE : (column + 1) * TILE],
+            (lambda: shared_act.append(gelu(pltpu.matmul_pop(acc)))) if k == depth - 1 else None,
+        )
+
+    stream([shared_up_job(c, k) for c in range(shared_units // TILE) for k in range(depth)])
+    shared_parts = []
+
+    def shared_down_job(column, k):
+        acc = small_accs[column % 2][column // 2]
+        last = k == shared_units // TILE - 1
+        return (
+            column % 2,
+            acc,
+            lambda: shared_act[k],
+            lambda: shared_down[k * TILE : (k + 1) * TILE, column * TILE : (column + 1) * TILE],
+            (lambda: shared_parts.append(pltpu.matmul_pop(acc))) if last else None,
+        )
+
+    stream(
+        [shared_down_job(c, k) for c in range(depth) for k in range(shared_units // TILE)]
+    )
+    shared = jnp.concatenate(shared_parts, axis=1)
+
+    def down_jobs(rows_ref, act_start, start, size):
+        def job(column, k):
+            return (
+                column % 2,
+                down_accs[column % 2][column // 2],
+                lambda: act_buf[:, act_start + k * TILE : act_start + (k + 1) * TILE],
+                lambda: rows_ref[
+                    start + k * TILE : start + (k + 1) * TILE,
+                    column * TILE : (column + 1) * TILE,
+                ],
+                None,
+            )
+
+        return [job(c, k) for c in range(depth) for k in range(size // TILE)]
+
     here = residuals[part_of(group, members)].astype(jnp.float32)
     token = lax.broadcasted_iota(jnp.int32, here.shape, 1)
     own_out[:blocks] = jnp.sum(jnp.where(token == member, here, 0.0), axis=1)
-    sums = jnp.dot(act_buf[:, :head], down_head[...], preferred_element_type=jnp.float32)
+    stream(down_jobs(down_head, 0, 0, head))
 
     routes_copy.wait()
     token_column = lax.broadcasted_iota(jnp.int32, (group_tokens, 1), 0)
     route = jnp.zeros((group_tokens, 1), jnp.int32)
     for index in range(group_tokens):
         route = jnp.where(token_column == index, routes[index], route)
-    expert_lane = lax.broadcasted_iota(jnp.int32, logits.shape, 1)
-    chosen = jnp.sum(jnp.where(expert_lane == route, logits, 0.0), axis=1, keepdims=True)
-    gate = jax.nn.sigmoid(chosen)
-    own_gate = jnp.sum(jnp.where(token_column == member, gate, 0.0), axis=0, keepdims=True)
+    router_rows = router[...].astype(jnp.float32)
+    expert_row = lax.broadcasted_iota(jnp.int32, router_rows.shape, 0)
+
+    def gate_for(expert):
+        picked = jnp.sum(jnp.where(expert_row == expert, router_rows, 0.0), axis=0, keepdims=True)
+        products = here_normed.astype(jnp.float32) * picked
+        return jax.nn.sigmoid(jnp.sum(products, axis=1, keepdims=True))
+
+    here_expert = member * groups + group
+    own_gate = jnp.sum(
+        jnp.where(token_column == member, gate_for(routes[member]), 0.0), axis=0, keepdims=True
+    )
     own_route = jnp.sum(jnp.where(token_column == member, route, 0), axis=0, keepdims=True)
     holder = lax.rem(own_route, groups)
     own_holder = holder * members + own_route // groups
@@ -331,13 +443,12 @@
     for size in pieces:
         for index in range(first // step_rows, (first + size) // step_rows):
             down_copy(index).wait()
-        sums = sums + jnp.dot(
-            act_buf[:, head + first : head + first + size],
-            down_buf[first : first + size],
-            preferred_element_type=jnp.float32,
-        )
+        stream(down_jobs(down_buf, head + first, first, size))
         first += size
-    here_gate = jnp.where(route == member * groups + group, gate, 0.0)
+    sums = jnp.concatenate(
+        [pltpu.matmul_pop(down_accs[column % 2][column // 2]) for column in range(depth)], axis=1
+    )
+    here_gate = jnp.where(route == here_expert, gate_for(here_expert), 0.0)
     parts = []
     for other in range(groups):
         rows = sums[other * group_tokens : (other + 1) * group_tokens]
@@ -378,10 +489,10 @@
     width, columns = expert_up.shape
     blocks = width // LANES
     columns = columns // lax.axis_size("group")
-    up_step, pieces = 1024, PIECES
+    pieces = PIECES
     rows = columns - down_head.shape[0]
     return pl.pallas_call(
-        functools.partial(mlp_kernel, ("group", "expert"), up_step, pieces),
+        functools.partial(mlp_kernel, ("group", "expert"), pieces),
         out_shape=(
             pltpu.VMEM((tokens, blocks, LANES), jnp.bfloat16),
             pltpu.VMEM((blocks + tokens, LANES), jnp.float32),
@@ -436,9 +547,19 @@
         out_specs=(VMEM, VMEM),
         scratch_shapes=[row] * 4 + [cache] * 2 + [pltpu.SemaphoreType.DMA((7,))],
         compiler_params=params(4),
-        cost_estimate=cost(10**11),
+        cost_estimate=cost(10**6),
         name="attend",
     )(lengths, query, key_new, value_new, key_cache, value_cache, hidden, expert_down)
+    message = pl.pallas_call(
+        hand_on_kernel,
+        out_shape=pltpu.VMEM(message.shape, message.dtype),
+        in_specs=[VMEM],
+        out_specs=VMEM,
+        input_output_aliases={0: 0},
+        compiler_params=params(2),
+        cost_estimate=cost(10**12),
+        name="hand_on",
+    )(message)
     gathered = lax.all_to_all(message, "expert", 0, 0)
     message = pl.pallas_call(
         project_kernel,

time: 46.8 us -> 46.7 us (level)
    pallas_call x1 -> x2, Pallas kernels: 7.31 us -> 7.1 us  [the longest x1 7.1 us: mlp(): pl.pallas_call(functools.partial(mlp_kernel, ('group', 'expert'), pieces)...]
where the time goes in v5:
time: 46.7 us; the launch traced here: 46.4 us
  blocking collectives  35 us (75%)
  Pallas kernels  10.7 us (23%)
  between operations  0.74 us (2%)
    all_to_all x1, blocking collectives, fast_body(): gathered = lax.all_to_all(message, 'expert', 0, 0)  14.9 us
    all_to_all x1, blocking collectives, fast_body(): residuals = lax.all_to_all(message, both, 0, 0)  10.2 us
    all_to_all x1, blocking collectives, fast_body(): terms = lax.all_to_all(terms, both, 0, 0)  9.94 us
    pallas_call x1, Pallas kernels, mlp(): pl.pallas_call(functools.partial(mlp_kernel, ('group', 'expert'), pieces)...  7.1 us
    pallas_call x1, Pallas kernels, fast_body(): pl.pallas_call(functools.partial(attend_kernel, 'group'), out_shape=(pltp...  2.42 us

profile of v5, /device:TPU:0, one launch (start us, length us, event | category | flops | bytes accessed | tf_op | source)
XLA Modules:
  0.0 46.4 jit_solution(11837962186541256388)
XLA Ops:
  0.7 2.4 %attend.1 = (bf16[16,24,128]{2,1,0:T(8,128)(2,1)S(1)}, bf16[512,2048]{1,0:T(8,128)(2,1)S(1)}) custom-call(s32[1]{0:T(128)S(6)} %copy.18.lengths, bf16[1,2048]{1,0:T(2,128)(2,1)} %query.1, bf16[1,2048]{1,0:T(2,128)(2,1)} %key_new.1, bf16[1,2048]{1,0:T(2,128)(2,1)} %value_new.1, bf16[1,256,2048]{2,1,0:T(8,128)(2,1)} %keys.1, bf16[1,256,2048]{2,1,0:T(8,128)(2,1)} %values.1, ...), custom_call_target="tpu_custom_call" | custom-call | flops 1000000 | bytes 3906 | tf_op jit(solution)/shard_map/attend/pallas_call | solution.py:540
  3.1 0.0 copy-start.1
  3.1 0.0 copy-start.2
  3.1 0.0 copy-start.3
  3.1 14.9 %all_to_all.15.gathered = bf16[16,24,128]{2,1,0:T(8,128)(2,1)S(1)} all-to-all(bf16[16,24,128]{2,1,0:T(8,128)(2,1)S(1)} %hand_on.1), channel_id=1, replica_groups=mesh['group'=2,'expert'=16] {'expert'}, dimensions={0} | all-to-all | bytes 196608 | tf_op jit(solution)/shard_map/all_to_all | solution.py:563
  18.0 0.0 copy-done.1
  18.0 0.0 copy-done.2
  18.0 0.0 copy-done.3
  18.0 0.0 copy-start
  18.0 0.0 copy-start.4
  18.0 0.0 copy-start.5
  18.0 0.5 %project.1 = bf16[32,16,128]{2,1,0:T(8,128)(2,1)S(1)} custom-call(bf16[16,24,128]{2,1,0:T(8,128)(2,1)S(1)} %all_to_all.15.gathered, bf16[2048,128]{1,0:T(8,128)(2,1)S(1)} %copy-done.3, bf16[2048,512]{1,0:T(8,128)(2,1)S(1)} %copy-done.1, bf16[512,2048]{1,0:T(8,128)(2,1)S(1)} %copy-done.2), custom_call_target="tpu_custom_call" | custom-call | flops 99999997952 | bytes 390624992 | tf_op jit(solution)/shard_map/project/pallas_call | solution.py:564
  18.5 10.2 %all_to_all.16.refs_1_ = bf16[32,16,128]{2,1,0:T(8,128)(2,1)S(1)} all-to-all(bf16[32,16,128]{2,1,0:T(8,128)(2,1)S(1)} %project.1), channel_id=1, replica_groups=mesh['group'=2,'expert'=16] {'group','expert'}, dimensions={0} | all-to-all | bytes 262144 | tf_op jit(solution)/shard_map/all_to_all | solution.py:573
  28.7 0.0 copy-done
  28.7 0.0 copy-done.4
  28.7 0.0 copy-done.5
  28.7 7.1 %mlp.1 = (bf16[32,16,128]{2,1,0:T(8,128)(2,1)S(1)}, f32[48,128]{1,0:T(8,128)S(1)}) custom-call(s32[16]{0:T(128)} %refs_0_.1, bf16[32,16,128]{2,1,0:T(8,128)(2,1)S(1)} %all_to_all.16.refs_1_, bf16[16,128]{1,0:T(8,128)(2,1)S(1)} %bitcast.3, bf16[32,2048]{1,0:T(8,128)(2,1)S(1)} %bitcast.2, bf16[2048,512]{1,0:T(8,128)(2,1)S(1)} %copy-done.1, ...), custom_call_target="tpu_custom_call" | custom-call | flops 99999997952 | bytes 390624992 | tf_op jit(solution)/shard_map/mlp/pallas_call | solution.py:494
  35.8 9.9 %all_to_all.17.terms = bf16[32,16,128]{2,1,0:T(8,128)(2,1)S(1)} all-to-all(bf16[32,16,128]{2,1,0:T(8,128)(2,1)S(1)} %get-tuple-element.11), channel_id=1, replica_groups=mesh['group'=2,'expert'=16] {'group','expert'}, dimensions={0} | all-to-all | bytes 262144 | tf_op jit(solution)/shard_map/all_to_all | solution.py:578
  45.8 0.7 %combine.1 = bf16[1,2048]{1,0:T(2,128)(2,1)} custom-call(bf16[32,16,128]{2,1,0:T(8,128)(2,1)S(1)} %all_to_all.17.terms, f32[48,128]{1,0:T(8,128)S(1)} %get-tuple-element.12.own), custom_call_target="tpu_custom_call" | custom-call | tf_op jit(solution)/shard_map/combine/pallas_call | solution.py:579
  (1 shorter events, 0.0 us)
Async XLA Ops:
  3.1 14.9 %copy-start.1 = (bf16[2048,512]{1,0:T(8,128)(2,1)S(1)}, bf16[2048,512]{1,0:T(8,128)(2,1)}, u32[]{:S(2)}) copy-start(bf16[2048,512]{1,0:T(8,128)(2,1)} %refs_4_.1) | copy-start | bytes 6291460
  3.1 14.9 %copy-start.2 = (bf16[512,2048]{1,0:T(8,128)(2,1)S(1)}, bf16[512,2048]{1,0:T(8,128)(2,1)}, u32[]{:S(2)}) copy-start(bf16[512,2048]{1,0:T(8,128)(2,1)} %refs_5_.1) | copy-start | bytes 6291460
  3.1 14.9 %copy-start.3 = (bf16[2048,128]{1,0:T(8,128)(2,1)S(1)}, bf16[2048,128]{1,0:T(8,128)(2,1)}, u32[]{:S(2)}) copy-start(bf16[2048,128]{1,0:T(8,128)(2,1)} %w_out.1) | copy-start | bytes 1572868
  18.0 10.7 %copy-start = (bf16[2048,8192]{1,0:T(8,128)(2,1)S(1)}, bf16[2048,8192]{1,0:T(8,128)(2,1)}, u32[]{:S(2)}) copy-start(bf16[2048,8192]{1,0:T(8,128)(2,1)} %refs_6_.1) | copy-start | bytes 100663296
  18.0 10.7 %copy-start.4 = (bf16[2048,32]{0,1:T(8,128)(2,1)S(1)}, bf16[2048,32]{0,1:T(8,128)(2,1)}, u32[]{:S(2)}) copy-start(bf16[2048,32]{0,1:T(8,128)(2,1)} %param.25) | copy-start | bytes 393220
  18.0 10.7 %copy-start.5 = (bf16[2048]{0:T(1024)(128)(2,1)S(1)}, bf16[2048]{0:T(1024)(128)(2,1)}, u32[]{:S(2)}) copy-start(bf16[2048]{0:T(1024)(128)(2,1)} %param.24) | copy-start | bytes 12292
